TPU v7x, 32 devices: a whole 2x2x4 slice. The times are simulated.
32 devices in a mesh: expert: 4 (over x, core), shard: 8 (over z, y).
Axes of the slice: x: 2, y: 2, z: 4, core: 2. Of those that a mesh axis runs over, the one named last changes fastest.
Arguments:
- tokens: bfloat16 [256, 4096], P(('expert', 'shard')), may hold values from -6 to 6
- router: bfloat16 [4096, 4], replicated, may hold values from -0.09375 to 0.09375
- expert_ids: int32 [256, 2], P(('expert', 'shard')), may hold values from 0 to 3, as said below
- w_gate: bfloat16 [4, 4096, 14336], P('expert', None, 'shard'), may hold values from -0.09375 to 0.09375
- w_up: bfloat16 [4, 4096, 14336], P('expert', None, 'shard'), may hold values from -0.09375 to 0.09375
- w_down: bfloat16 [4, 14336, 4096], P('expert', 'shard'), may hold values from -0.046875 to 0.046875
Outputs:
- mixed: bfloat16 [256, 4096], P(('expert', 'shard'))
Inputs may be any that keep to these rules, and one draw needn't show every extreme that they name: `expert_ids`: each row names 2 different experts. Within the rows of one device no expert is named more than 4 times, and on every device some expert is named exactly 4 times.
All inputs are finite; a program needn't handle non-finite values.
Results may differ from a plain program's by a relative error of at most 0.0074.
Values may be sent and summed in bfloat16 or wider, within the bound.
No kernel may reach another device: no remote copies, remote signals or barrier semaphores. Data moves between devices by JAX's collectives and lax.ppermute only.
A program may use at most 128 MiB of HBM per device.

v0:
```python
import functools

import jax
import jax.numpy as jnp
from jax import lax
from jax.experimental import pallas as pl
from jax.experimental.pallas import tpu as pltpu
from jax.sharding import PartitionSpec as P


LANES = 128
HIDDEN_TILE = 256
OUT_TILE = 1024
LONG = 2e10
MIB = 1 << 20


def cost(flops, moved):
    return pl.CostEstimate(flops=int(flops), bytes_accessed=int(moved), transcendentals=0)


def dot(a, b, contract=(1, 0)):
    dims = (((contract[0],), (contract[1],)), ((), ()))
    return lax.dot_general(a, b, dims, preferred_element_type=jnp.float32)


def line_split(count):
    inner = 1
    while inner * inner * 4 <= count:
        inner *= 2
    return count // inner, inner


def swap(value, experts, shards, expert_bits, shard_bits):
    pairs = [
        (e * shards + s, (e ^ expert_bits) * shards + (s ^ shard_bits))
        for e in range(experts)
        for s in range(shards)
    ]
    return lax.ppermute(value, ("expert", "shard"), pairs)


def picks(ids_by_lane, first_expert, n_experts, blocks, slots_per):
    per_block = 2 * slots_per
    n_tokens = blocks * per_block
    rows = n_experts * blocks * slots_per
    row = lax.broadcasted_iota(jnp.int32, (rows, n_tokens), 0)
    token = lax.broadcasted_iota(jnp.int32, (rows, n_tokens), 1)
    expert = (first_expert ^ (row // (blocks * slots_per))).astype(jnp.float32)
    block = (row // slots_per) % blocks
    slot = (row % slots_per).astype(jnp.float32)
    is_first = ids_by_lane[0:1, :] == expert
    names = jnp.where(is_first | (ids_by_lane[1:2, :] == expert), 1.0, 0.0)
    earlier_token = lax.broadcasted_iota(jnp.int32, (n_tokens, n_tokens), 0)
    later_token = lax.broadcasted_iota(jnp.int32, (n_tokens, n_tokens), 1)
    earlier = jnp.where(
        (earlier_token < later_token)
        & (earlier_token // per_block == later_token // per_block),
        1.0,
        0.0,
    )
    before = dot(names.astype(jnp.bfloat16), earlier.astype(jnp.bfloat16))
    chosen = jnp.where((token // per_block == block) & (before == slot), names, 0.0)
    return chosen, is_first


def ids_to_lanes(packed_ids, blocks):
    n_tokens = packed_ids.shape[0]
    per_block = n_tokens // blocks
    lane = lax.broadcasted_iota(jnp.int32, (LANES, n_tokens), 0)
    token = lax.broadcasted_iota(jnp.int32, (LANES, n_tokens), 1)
    row = lax.broadcasted_iota(jnp.int32, (per_block, n_tokens), 1)
    lanes = jnp.zeros((per_block, n_tokens), jnp.float32)
    spread = jnp.where(lane == token % per_block, 1.0, 0.0).astype(jnp.bfloat16)
    spreads = dot(packed_ids, spread)
    for block in range(blocks):
        mine = spreads[block * per_block : (block + 1) * per_block]
        lanes = lanes + jnp.where(row // per_block == block, mine, 0.0)
    return lanes


def gather_blocks(refs):
    return jnp.concatenate([ref[...].astype(jnp.float32) for ref in refs], axis=0).astype(
        jnp.bfloat16
    )


def dispatch_kernel(blocks, n_experts, width, *refs):
    packed = gather_blocks(refs[:blocks])
    out_refs = refs[blocks:]
    slots_per = packed.shape[0] // blocks // 2
    per_expert = blocks * slots_per
    lanes = ids_to_lanes(packed[:, width:], blocks)
    chosen, _ = picks(lanes, lax.axis_index("expert"), n_experts, blocks, slots_per)
    rows = dot(chosen.astype(jnp.bfloat16), packed[:, :width]).astype(jnp.bfloat16)
    for k in range(n_experts):
        out_refs[k][...] = rows[k * per_expert : (k + 1) * per_expert]


def pack_kernel(tokens_ref, ids_ref, packed_ref):
    n_tokens, width = tokens_ref.shape
    packed_ref[:, :width] = tokens_ref[...]
    lane = lax.broadcasted_iota(jnp.int32, (LANES, n_tokens), 0)
    token = lax.broadcasted_iota(jnp.int32, (LANES, n_tokens), 1)
    spread = jnp.where(lane == token, 1.0, 0.0).astype(jnp.bfloat16)
    ids = ids_ref[...].astype(jnp.float32).astype(jnp.bfloat16)
    rows = jnp.concatenate([ids, jnp.zeros((n_tokens - 2, n_tokens), jnp.bfloat16)], axis=0)
    packed_ref[:, width:] = dot(rows, spread, (1, 1)).astype(jnp.bfloat16)


def gates_kernel(blocks, n_experts, width, *refs):
    router_ref, high_ref, low_ref = refs[blocks:]
    packed = gather_blocks(refs[:blocks])
    slots_per = packed.shape[0] // blocks // 2
    lanes = ids_to_lanes(packed[:, width:], blocks)
    chosen, is_first = picks(lanes, lax.axis_index("expert"), n_experts, blocks, slots_per)
    logits = dot(router_ref[...], packed[:, :width], (1, 1))
    expert = lax.broadcasted_iota(jnp.int32, logits.shape, 0).astype(jnp.float32)
    first = jnp.sum(jnp.where(lanes[0:1, :] == expert, logits, 0.0), axis=0, keepdims=True)
    second = jnp.sum(jnp.where(lanes[1:2, :] == expert, logits, 0.0), axis=0, keepdims=True)
    gate = 1.0 / (1.0 + jnp.exp(-(first - second)))
    weights = chosen * jnp.where(is_first, gate, 1.0 - gate)
    high = weights.astype(jnp.bfloat16)
    high_ref[...] = high
    low_ref[...] = (weights - high.astype(jnp.float32)).astype(jnp.bfloat16)


def ffn_kernel(parts, tile_width, out_tile, *refs):
    row_refs = refs[:parts]
    gate_ref, up_ref, down_ref = refs[parts : parts + 3]
    out_refs = refs[parts + 3 : 2 * parts + 3]
    rows, hidden = refs[2 * parts + 3 :]
    per_part = row_refs[0].shape[0]
    for part in range(parts):
        rows[pl.ds(part * per_part, per_part), :] = row_refs[part][...]

    @pl.loop(0, hidden.shape[1] // tile_width)
    def _(tile):
        columns = pl.ds(pl.multiple_of(tile * tile_width, tile_width), tile_width)
        gate = dot(rows[...], gate_ref[:, columns])
        up = dot(rows[...], up_ref[:, columns])
        hidden[:, columns] = (gate / (1.0 + jnp.exp(-gate)) * up).astype(jnp.bfloat16)

    @pl.loop(0, down_ref.shape[1] // out_tile)
    def _(tile):
        columns = pl.ds(pl.multiple_of(tile * out_tile, out_tile), out_tile)
        result = dot(hidden[...], down_ref[:, columns]).astype(jnp.bfloat16)
        for part in range(parts):
            out_refs[part][:, columns] = result[part * per_part : (part + 1) * per_part]


def combine_kernel(parts, n_experts, blocks, *refs):
    part_refs = refs[:parts]
    high_ref, low_ref = refs[parts : parts + 2]
    out_refs = refs[parts + 2 :]
    inner = parts // n_experts
    rows = jnp.concatenate([ref[...] for ref in part_refs], axis=0)
    high = jnp.concatenate([high_ref[...]] * inner, axis=0)
    low = jnp.concatenate([low_ref[...]] * inner, axis=0)
    mixed = dot(high, rows, (0, 0)) + dot(low, rows, (0, 0))
    per_block = mixed.shape[0] // blocks
    for block in range(blocks):
        out_refs[block][...] = mixed[block * per_block : (block + 1) * per_block].astype(
            jnp.bfloat16
        )


def final_kernel(*refs):
    total = refs[0][...].astype(jnp.float32)
    for ref in refs[1:-1]:
        total = total + ref[...].astype(jnp.float32)
    refs[-1][...] = total.astype(jnp.bfloat16)


def shards_program(n_expert_axis, n_shard_axis, tokens, router, expert_ids, w_gate, w_up, w_down):
    local_tokens, width = tokens.shape
    n_experts = router.shape[1]
    outer, inner = line_split(n_shard_axis)
    slots_per = local_tokens // 2
    per_expert = outer * slots_per
    parts = inner * n_experts
    n_rows = parts * per_expert
    gathered = outer * local_tokens
    n_hidden = w_gate.shape[2]
    bf16 = jnp.bfloat16
    vmem = pl.BlockSpec(memory_space=pltpu.VMEM)
    hbm = pl.BlockSpec(memory_space=pltpu.HBM)

    def exchange(value, expert_bits, shard_bits):
        return swap(value, n_expert_axis, n_shard_axis, expert_bits, shard_bits)

    w_gate, w_up, w_down = w_gate[0], w_up[0], w_down[0]
    packed = pl.pallas_call(
        pack_kernel,
        name="pack",
        out_shape=jax.ShapeDtypeStruct((local_tokens, width + LANES), bf16),
        in_specs=[vmem] * 2,
        out_specs=vmem,
        compiler_params=pltpu.CompilerParams(vmem_limit_bytes=2 * MIB),
        cost_estimate=cost(LONG, MIB),
    )(*(pltpu.with_memory_space_constraint(v, pltpu.HBM) for v in (tokens, expert_ids.T)))
    along = [packed] + [exchange(packed, 0, d * inner) for d in range(1, outer)]

    tile_width = HIDDEN_TILE if n_hidden % HIDDEN_TILE == 0 else LANES
    buffers = pl.pallas_call(
        functools.partial(dispatch_kernel, outer, n_experts, width),
        name="dispatch",
        out_shape=[jax.ShapeDtypeStruct((per_expert, width), bf16)] * n_experts,
        in_specs=[vmem] * outer,
        out_specs=[vmem] * n_experts,
        compiler_params=pltpu.CompilerParams(vmem_limit_bytes=6 * MIB),
        cost_estimate=cost(LONG, 4 * MIB),
    )(*along)

    order = [(i, k) for i in range(inner) for k in range(n_experts)]
    row_parts = [buffers[k] if (i, k) == (0, 0) else exchange(buffers[k], k, i) for i, k in order]

    high, low = pl.pallas_call(
        functools.partial(gates_kernel, outer, n_experts, width),
        name="gates",
        out_shape=[jax.ShapeDtypeStruct((n_experts * per_expert, gathered), bf16)] * 2,
        in_specs=[vmem] * (outer + 1),
        out_specs=[vmem] * 2,
        compiler_params=pltpu.CompilerParams(vmem_limit_bytes=6 * MIB),
        cost_estimate=cost(LONG, MIB),
    )(*along, router.T)

    out_parts = pl.pallas_call(
        functools.partial(ffn_kernel, parts, tile_width, OUT_TILE),
        name="ffn",
        out_shape=[jax.ShapeDtypeStruct((per_expert, width), bf16)] * parts,
        in_specs=[vmem] * (parts + 3),
        out_specs=[vmem] * parts,
        scratch_shapes=[pltpu.VMEM((n_rows, width), bf16), pltpu.VMEM((n_rows, n_hidden), bf16)],
        compiler_params=pltpu.CompilerParams(vmem_limit_bytes=5 * MIB),
        cost_estimate=cost(6 * n_rows * width * n_hidden, 6 * width * n_hidden),
    )(*row_parts, w_gate, w_up, w_down)

    back = [
        out_parts[j] if (i, k) == (0, 0) else exchange(out_parts[j], k, i)
        for j, (i, k) in enumerate(order)
    ]
    mixed = pl.pallas_call(
        functools.partial(combine_kernel, parts, n_experts, outer),
        name="combine",
        out_shape=[jax.ShapeDtypeStruct((local_tokens, width), bf16)] * outer,
        in_specs=[vmem] * (parts + 2),
        out_specs=[vmem] * outer,
        compiler_params=pltpu.CompilerParams(vmem_limit_bytes=20 * MIB),
        cost_estimate=cost(4 * n_rows * gathered * width, 4 * MIB),
    )(*back, high, low)
    home = [mixed[0]] + [exchange(mixed[d], 0, d * inner) for d in range(1, outer)]
    return pl.pallas_call(
        final_kernel,
        name="final",
        out_shape=jax.ShapeDtypeStruct((local_tokens, width), bf16),
        in_specs=[vmem] * outer,
        out_specs=vmem,
        compiler_params=pltpu.CompilerParams(vmem_limit_bytes=4 * MIB),
        cost_estimate=cost(1e6, MIB),
    )(*home)


def solution(mesh):
    placed = (
        P(("expert", "shard"), None),
        P(),
        P(("expert", "shard"), None),
        P("expert", None, "shard"),
        P("expert", None, "shard"),
        P("expert", "shard", None),
    )
    experts, shards = mesh.shape["expert"], mesh.shape["shard"]

    def body(*args):
        return shards_program(experts, shards, *args)

    return jax.shard_map(
        body, mesh=mesh, in_specs=placed, out_specs=P(("expert", "shard"), None), check_vma=False
    )
```

profile of v0, /device:TPU:0, one launch (start us, length us, event | category | flops | bytes accessed | tf_op | source)
XLA Modules:
  0.0 63.9 jit_solution(17274525538224964882)
XLA Ops:
  0.0 0.0 slice-start.9
  0.0 1.1 %pack.1.refs_0_ = bf16[8,4224]{1,0:T(8,128)(2,1)S(1)} custom-call(bf16[8,4096]{1,0:T(8,128)(2,1)} %tokens_ref.1, s32[2,8]{1,0:T(2,128)} %bitcast.15), custom_call_target="tpu_custom_call" | custom-call | flops 20000000000 | bytes 1048576 | tf_op jit(solution)/shard_map/pack/pallas_call | solution.py:193
  1.2 0.0 slice-start.7
  1.2 0.0 slice-start.10
  1.2 0.0 slice-start.11
  1.2 5.2 %collective-permute-start.2 = (bf16[8,4224]{1,0:T(8,128)(2,1)S(1)}, bf16[8,4224]{1,0:T(8,128)(2,1)S(1)}, u32[]{:S(2)}, u32[]{:S(2)}) collective-permute-start(bf16[8,4224]{1,0:T(8,128)(2,1)S(1)} %pack.1.refs_0_), channel_id=1, source_target_pairs={{0,6},{1,7},{2,4},{3,5},{4,2},{5,3},{6,0},{7,1},{8,14},{9,15},{10,... | collective-permute-start | bytes 202760 | tf_op jit(solution)/shard_map/ppermute | solution.py:40
  6.4 0.0 collective-permute-start.1
  6.4 0.6 %collective-permute-start = (bf16[8,4224]{1,0:T(8,128)(2,1)S(1)}, bf16[8,4224]{1,0:T(8,128)(2,1)S(1)}, u32[]{:S(2)}, u32[]{:S(2)}) collective-permute-start(bf16[8,4224]{1,0:T(8,128)(2,1)S(1)} %pack.1.refs_0_), channel_id=1, source_target_pairs={{0,2},{1,3},{2,0},{3,1},{4,6},{5,7},{6,4},{7,5},{8,10},{9,11},{10,... | collective-permute-start | bytes 202760 | tf_op jit(solution)/shard_map/ppermute | solution.py:40
  7.0 1.9 %collective-permute-done.2.refs_3_ = bf16[8,4224]{1,0:T(8,128)(2,1)S(1)} collective-permute-done((bf16[8,4224]{1,0:T(8,128)(2,1)S(1)}, bf16[8,4224]{1,0:T(8,128)(2,1)S(1)}, u32[]{:S(2)}, u32[]{:S(2)}) %collective-permute-start.2) | collective-permute-done | bytes 67616 | tf_op jit(solution)/shard_map/ppermute | solution.py:40
  8.9 3.2 %collective-permute-done.1.refs_2_ = bf16[8,4224]{1,0:T(8,128)(2,1)S(1)} collective-permute-done((bf16[8,4224]{1,0:T(8,128)(2,1)S(1)}, bf16[8,4224]{1,0:T(8,128)(2,1)S(1)}, u32[]{:S(2)}, u32[]{:S(2)}) %collective-permute-start.1) | collective-permute-done | bytes 67616 | tf_op jit(solution)/shard_map/ppermute | solution.py:40
  12.1 0.0 collective-permute-done.refs_1_
  12.1 0.5 dispatch.1
  12.6 1.6 %collective-permute-start.6 = (bf16[16,4096]{1,0:T(8,128)(2,1)S(1)}, bf16[16,4096]{1,0:T(8,128)(2,1)S(1)}, u32[]{:S(2)}, u32[]{:S(2)}) collective-permute-start(bf16[16,4096]{1,0:T(8,128)(2,1)S(1)} %get-tuple-element.23.refs_0_), channel_id=1, source_target_pairs={{0,1},{1,0},{2,3},{3,2},{4,5},{5,4},{6,7},{7,6},{8,9},{9,8},{10,11... | collective-permute-start | bytes 393224 | tf_op jit(solution)/shard_map/ppermute | solution.py:40
  14.2 0.0 collective-permute-start.7
  14.2 0.6 collective-permute-start.3
  14.9 2.4 %collective-permute-start.8 = (bf16[16,4096]{1,0:T(8,128)(2,1)S(1)}, bf16[16,4096]{1,0:T(8,128)(2,1)S(1)}, u32[]{:S(2)}, u32[]{:S(2)}) collective-permute-start(bf16[16,4096]{1,0:T(8,128)(2,1)S(1)} %get-tuple-element.25), channel_id=1, source_target_pairs={{0,17},{1,16},{2,19},{3,18},{4,21},{5,20},{6,23},{7,22},{8,25},{9,... | collective-permute-start | bytes 393224 | tf_op jit(solution)/shard_map/ppermute | solution.py:40
  17.3 0.5 collective-permute-start.4
  17.8 2.3 %collective-permute-done.6.refs_4_ = bf16[16,4096]{1,0:T(8,128)(2,1)S(1)} collective-permute-done((bf16[16,4096]{1,0:T(8,128)(2,1)S(1)}, bf16[16,4096]{1,0:T(8,128)(2,1)S(1)}, u32[]{:S(2)}, u32[]{:S(2)}) %collective-permute-start.6) | collective-permute-done | bytes 131104 | tf_op jit(solution)/shard_map/ppermute | solution.py:40
  20.1 0.0 collective-permute-start.9
  20.2 2.7 %collective-permute-done.7.refs_5_ = bf16[16,4096]{1,0:T(8,128)(2,1)S(1)} collective-permute-done((bf16[16,4096]{1,0:T(8,128)(2,1)S(1)}, bf16[16,4096]{1,0:T(8,128)(2,1)S(1)}, u32[]{:S(2)}, u32[]{:S(2)}) %collective-permute-start.7) | collective-permute-done | bytes 131104 | tf_op jit(solution)/shard_map/ppermute | solution.py:40
  22.8 1.8 %collective-permute-start.5 = (bf16[16,4096]{1,0:T(8,128)(2,1)S(1)}, bf16[16,4096]{1,0:T(8,128)(2,1)S(1)}, u32[]{:S(2)}, u32[]{:S(2)}) collective-permute-start(bf16[16,4096]{1,0:T(8,128)(2,1)S(1)} %get-tuple-element.26), channel_id=1, source_target_pairs={{0,24},{1,25},{2,26},{3,27},{4,28},{5,29},{6,30},{7,31},{8,16},{9,... | collective-permute-start | bytes 393224 | tf_op jit(solution)/shard_map/ppermute | solution.py:40
  24.7 0.0 collective-permute-done.3.refs_1_
  24.7 0.0 collective-permute-done.8.refs_6_
  24.7 0.8 %collective-permute-done.9.refs_7_ = bf16[16,4096]{1,0:T(8,128)(2,1)S(1)} collective-permute-done((bf16[16,4096]{1,0:T(8,128)(2,1)S(1)}, bf16[16,4096]{1,0:T(8,128)(2,1)S(1)}, u32[]{:S(2)}, u32[]{:S(2)}) %collective-permute-start.9) | collective-permute-done | bytes 131104 | tf_op jit(solution)/shard_map/ppermute | solution.py:40
  25.4 3.9 %collective-permute-done.5.refs_3_ = bf16[16,4096]{1,0:T(8,128)(2,1)S(1)} collective-permute-done((bf16[16,4096]{1,0:T(8,128)(2,1)S(1)}, bf16[16,4096]{1,0:T(8,128)(2,1)S(1)}, u32[]{:S(2)}, u32[]{:S(2)}) %collective-permute-start.5) | collective-permute-done | bytes 131104 | tf_op jit(solution)/shard_map/ppermute | solution.py:40
  29.5 0.0 copy-start
  29.5 8.1 %ffn.1 = (bf16[16,4096]{1,0:T(8,128)(2,1)S(1)}, bf16[16,4096]{1,0:T(8,128)(2,1)S(1)}, bf16[16,4096]{1,0:T(8,128)(2,1)S(1)}, bf16[16,4096]{1,0:T(8,128)(2,1)S(1)}...) custom-call(bf16[16,4096]{1,0:T(8,128)(2,1)S(1)} %get-tuple-element., ...), custom_call_target="tpu_custom_call" | custom-call | flops 5637144576 | bytes 44040192 | tf_op jit(solution)/shard_map/ffn/pallas_call | solution.py:228
  37.6 0.3 collective-permute-start.10
  37.8 1.8 %collective-permute-start.11 = (bf16[16,4096]{1,0:T(8,128)(2,1)S(1)}, bf16[16,4096]{1,0:T(8,128)(2,1)S(1)}, u32[]{:S(2)}, u32[]{:S(2)}) collective-permute-start(bf16[16,4096]{1,0:T(8,128)(2,1)S(1)} %get-tuple-element.29), channel_id=1, source_target_pairs={{0,16},{1,17},{2,18},{3,19},{4,20},{5,21},{6,22},{7,23},{8,24},{9,... | collective-permute-start | bytes 393224 | tf_op jit(solution)/shard_map/ppermute | solution.py:40
  39.6 0.0 collective-permute-start.12
  39.6 0.4 collective-permute-start.13
  40.1 1.3 %collective-permute-start.14 = (bf16[16,4096]{1,0:T(8,128)(2,1)S(1)}, bf16[16,4096]{1,0:T(8,128)(2,1)S(1)}, u32[]{:S(2)}, u32[]{:S(2)}) collective-permute-start(bf16[16,4096]{1,0:T(8,128)(2,1)S(1)} %get-tuple-element.32), channel_id=1, source_target_pairs={{0,9},{1,8},{2,11},{3,10},{4,13},{5,12},{6,15},{7,14},{8,1},{9,0},... | collective-permute-start | bytes 393224 | tf_op jit(solution)/shard_map/ppermute | solution.py:40
  41.3 0.0 collective-permute-done.10.refs_1_
  41.3 1.7 %collective-permute-start.15 = (bf16[16,4096]{1,0:T(8,128)(2,1)S(1)}, bf16[16,4096]{1,0:T(8,128)(2,1)S(1)}, u32[]{:S(2)}, u32[]{:S(2)}) collective-permute-start(bf16[16,4096]{1,0:T(8,128)(2,1)S(1)} %get-tuple-element.33), channel_id=1, source_target_pairs={{0,17},{1,16},{2,19},{3,18},{4,21},{5,20},{6,23},{7,22},{8,25},{9,... | collective-permute-start | bytes 393224 | tf_op jit(solution)/shard_map/ppermute | solution.py:40
  43.0 1.2 %collective-permute-done.11.refs_2_ = bf16[16,4096]{1,0:T(8,128)(2,1)S(1)} collective-permute-done((bf16[16,4096]{1,0:T(8,128)(2,1)S(1)}, bf16[16,4096]{1,0:T(8,128)(2,1)S(1)}, u32[]{:S(2)}, u32[]{:S(2)}) %collective-permute-start.11) | collective-permute-done | bytes 131104 | tf_op jit(solution)/shard_map/ppermute | solution.py:40
  44.2 0.1 collective-permute-start.16
  44.3 0.3 gates.1
  44.7 1.6 %collective-permute-done.12.refs_3_ = bf16[16,4096]{1,0:T(8,128)(2,1)S(1)} collective-permute-done((bf16[16,4096]{1,0:T(8,128)(2,1)S(1)}, bf16[16,4096]{1,0:T(8,128)(2,1)S(1)}, u32[]{:S(2)}, u32[]{:S(2)}) %collective-permute-start.12) | collective-permute-done | bytes 131104 | tf_op jit(solution)/shard_map/ppermute | solution.py:40
  46.3 0.0 collective-permute-done.13.refs_4_
  46.3 6.9 %collective-permute-done.14.refs_5_ = bf16[16,4096]{1,0:T(8,128)(2,1)S(1)} collective-permute-done((bf16[16,4096]{1,0:T(8,128)(2,1)S(1)}, bf16[16,4096]{1,0:T(8,128)(2,1)S(1)}, u32[]{:S(2)}, u32[]{:S(2)}) %collective-permute-start.14) | collective-permute-done | bytes 131104 | tf_op jit(solution)/shard_map/ppermute | solution.py:40
  53.2 0.4 combine.1
  53.6 1.1 %collective-permute-start.17 = (bf16[8,4096]{1,0:T(8,128)(2,1)S(1)}, bf16[8,4096]{1,0:T(8,128)(2,1)S(1)}, u32[]{:S(2)}, u32[]{:S(2)}) collective-permute-start(bf16[8,4096]{1,0:T(8,128)(2,1)S(1)} %get-tuple-element.38), channel_id=1, source_target_pairs={{0,2},{1,3},{2,0},{3,1},{4,6},{5,7},{6,4},{7,5},{8,10},{9,11},{10,... | collective-permute-start | bytes 196616 | tf_op jit(solution)/shard_map/ppermute | solution.py:40
  54.7 2.2 %collective-permute-start.18 = (bf16[8,4096]{1,0:T(8,128)(2,1)S(1)}, bf16[8,4096]{1,0:T(8,128)(2,1)S(1)}, u32[]{:S(2)}, u32[]{:S(2)}) collective-permute-start(bf16[8,4096]{1,0:T(8,128)(2,1)S(1)} %get-tuple-element.39), channel_id=1, source_target_pairs={{0,4},{1,5},{2,6},{3,7},{4,0},{5,1},{6,2},{7,3},{8,12},{9,13},{10,... | collective-permute-start | bytes 196616 | tf_op jit(solution)/shard_map/ppermute | solution.py:40
  57.0 1.1 %collective-permute-start.19 = (bf16[8,4096]{1,0:T(8,128)(2,1)S(1)}, bf16[8,4096]{1,0:T(8,128)(2,1)S(1)}, u32[]{:S(2)}, u32[]{:S(2)}) collective-permute-start(bf16[8,4096]{1,0:T(8,128)(2,1)S(1)} %get-tuple-element.40), channel_id=1, source_target_pairs={{0,6},{1,7},{2,4},{3,5},{4,2},{5,3},{6,0},{7,1},{8,14},{9,15},{10,... | collective-permute-start | bytes 196616 | tf_op jit(solution)/shard_map/ppermute | solution.py:40
  58.1 0.1 collective-permute-done.17.refs_1_
  58.2 5.1 %collective-permute-done.18.refs_2_ = bf16[8,4096]{1,0:T(8,128)(2,1)S(1)} collective-permute-done((bf16[8,4096]{1,0:T(8,128)(2,1)S(1)}, bf16[8,4096]{1,0:T(8,128)(2,1)S(1)}, u32[]{:S(2)}, u32[]{:S(2)}) %collective-permute-start.18) | collective-permute-done | bytes 65568 | tf_op jit(solution)/shard_map/ppermute | solution.py:40
  63.2 0.0 collective-permute-done.19.refs_3_
  63.2 0.7 %final.1 = bf16[8,4096]{1,0:T(8,128)(2,1)} custom-call(bf16[8,4096]{1,0:T(8,128)(2,1)S(1)} %get-tuple-element.37.refs_0_, bf16[8,4096]{1,0:T(8,128)(2,1)S(1)} %collective-permute-done.17.refs_1_, bf16[8,4096]{1,0:T(8,128)(2,1)S(1)} %collective-permute-done.18.refs_2_, bf16[8,4096]{1,0:T(8,128)(2,1)S(1)} %collective-permute-done.19.refs_3_), custom_call_target="tpu_custom_call" | custom-call | flops 1000000 | bytes 1048576 | tf_op jit(solution)/shard_map/final/pallas_call | solution.py:253
  (27 shorter events, 0.0 us)
Async XLA Ops:
  0.0 29.4 %slice-start = ((s8[14680064]{0:T(1024)(128)(4,1)}), s8[4194304]{0:T(1024)(128)(4,1)S(1)}, s32[]{:S(2)}) async-start(s8[14680064]{0:T(1024)(128)(4,1)} %bitcast.5), calls=%async_computation | async-start | bytes 8388608
  0.0 29.4 %slice-start.1 = ((s8[14680064]{0:T(1024)(128)(4,1)}), s8[4194304]{0:T(1024)(128)(4,1)S(1)}, s32[]{:S(2)}) async-start(s8[14680064]{0:T(1024)(128)(4,1)} %bitcast.5), calls=%async_computation.1 | async-start | bytes 8388608
  0.0 29.4 %slice-start.4 = ((s8[14680064]{0:T(1024)(128)(4,1)}), s8[4194304]{0:T(1024)(128)(4,1)S(1)}, s32[]{:S(2)}) async-start(s8[14680064]{0:T(1024)(128)(4,1)} %bitcast.8), calls=%async_computation.4 | async-start | bytes 8388608
  0.0 29.4 %slice-start.5 = ((s8[14680064]{0:T(1024)(128)(4,1)}), s8[4194304]{0:T(1024)(128)(4,1)S(1)}, s32[]{:S(2)}) async-start(s8[14680064]{0:T(1024)(128)(4,1)} %bitcast.8), calls=%async_computation.5 | async-start | bytes 8388608
  0.0 29.4 %slice-start.8 = ((s8[14680064]{0:T(1024)(128)(4,1)}), s8[4194304]{0:T(1024)(128)(4,1)S(1)}, s32[]{:S(2)}) async-start(s8[14680064]{0:T(1024)(128)(4,1)} %bitcast.11), calls=%async_computation.8 | async-start | bytes 8388608
  0.0 29.4 %slice-start.9 = ((s8[14680064]{0:T(1024)(128)(4,1)}), s8[4194304]{0:T(1024)(128)(4,1)S(1)}, s32[]{:S(2)}) async-start(s8[14680064]{0:T(1024)(128)(4,1)} %bitcast.11), calls=%async_computation.9 | async-start | bytes 8388608
  1.2 28.3 %slice-start.2 = ((s8[14680064]{0:T(1024)(128)(4,1)}), s8[4194304]{0:T(1024)(128)(4,1)S(1)}, s32[]{:S(2)}) async-start(s8[14680064]{0:T(1024)(128)(4,1)} %bitcast.5), calls=%async_computation.2 | async-start | bytes 8388608
  1.2 28.3 %slice-start.3 = ((s8[14680064]{0:T(1024)(128)(4,1)}), s8[2097152]{0:T(1024)(128)(4,1)S(1)}, s32[]{:S(2)}) async-start(s8[14680064]{0:T(1024)(128)(4,1)} %bitcast.5), calls=%async_computation.3 | async-start | bytes 4194304
  1.2 28.3 %slice-start.6 = ((s8[14680064]{0:T(1024)(128)(4,1)}), s8[4194304]{0:T(1024)(128)(4,1)S(1)}, s32[]{:S(2)}) async-start(s8[14680064]{0:T(1024)(128)(4,1)} %bitcast.8), calls=%async_computation.6 | async-start | bytes 8388608
  1.2 28.3 %slice-start.7 = ((s8[14680064]{0:T(1024)(128)(4,1)}), s8[2097152]{0:T(1024)(128)(4,1)S(1)}, s32[]{:S(2)}) async-start(s8[14680064]{0:T(1024)(128)(4,1)} %bitcast.8), calls=%async_computation.7 | async-start | bytes 4194304
  1.2 28.3 %slice-start.10 = ((s8[14680064]{0:T(1024)(128)(4,1)}), s8[4194304]{0:T(1024)(128)(4,1)S(1)}, s32[]{:S(2)}) async-start(s8[14680064]{0:T(1024)(128)(4,1)} %bitcast.11), calls=%async_computation.10 | async-start | bytes 8388608
  1.2 28.3 %slice-start.11 = ((s8[14680064]{0:T(1024)(128)(4,1)}), s8[2097152]{0:T(1024)(128)(4,1)S(1)}, s32[]{:S(2)}) async-start(s8[14680064]{0:T(1024)(128)(4,1)} %bitcast.11), calls=%async_computation.11 | async-start | bytes 4194304
  1.2 7.7 %collective-permute-start.2 = (bf16[8,4224]{1,0:T(8,128)(2,1)S(1)}, bf16[8,4224]{1,0:T(8,128)(2,1)S(1)}, u32[]{:S(2)}, u32[]{:S(2)}) collective-permute-start(bf16[8,4224]{1,0:T(8,128)(2,1)S(1)} %pack.1.refs_0_), channel_id=1, source_target_pairs={{0,6},{1,7},{2,4},{3,5},{4,2},{5,3},{6,0},{7,1},{8,14},{9,15},{10,... | collective-permute-start | bytes 202760 | tf_op jit(solution)/shard_map/ppermute | solution.py:40
  6.4 5.8 %collective-permute-start.1 = (bf16[8,4224]{1,0:T(8,128)(2,1)S(1)}, bf16[8,4224]{1,0:T(8,128)(2,1)S(1)}, u32[]{:S(2)}, u32[]{:S(2)}) collective-permute-start(bf16[8,4224]{1,0:T(8,128)(2,1)S(1)} %pack.1.refs_0_), channel_id=1, source_target_pairs={{0,4},{1,5},{2,6},{3,7},{4,0},{5,1},{6,2},{7,3},{8,12},{9,13},{10,... | collective-permute-start | bytes 202760 | tf_op jit(solution)/shard_map/ppermute | solution.py:40
  6.4 5.8 %collective-permute-start = (bf16[8,4224]{1,0:T(8,128)(2,1)S(1)}, bf16[8,4224]{1,0:T(8,128)(2,1)S(1)}, u32[]{:S(2)}, u32[]{:S(2)}) collective-permute-start(bf16[8,4224]{1,0:T(8,128)(2,1)S(1)} %pack.1.refs_0_), channel_id=1, source_target_pairs={{0,2},{1,3},{2,0},{3,1},{4,6},{5,7},{6,4},{7,5},{8,10},{9,11},{10,... | collective-permute-start | bytes 202760 | tf_op jit(solution)/shard_map/ppermute | solution.py:40
  12.6 7.5 %collective-permute-start.6 = (bf16[16,4096]{1,0:T(8,128)(2,1)S(1)}, bf16[16,4096]{1,0:T(8,128)(2,1)S(1)}, u32[]{:S(2)}, u32[]{:S(2)}) collective-permute-start(bf16[16,4096]{1,0:T(8,128)(2,1)S(1)} %get-tuple-element.23.refs_0_), channel_id=1, source_target_pairs={{0,1},{1,0},{2,3},{3,2},{4,5},{5,4},{6,7},{7,6},{8,9},{9,8},{10,11... | collective-permute-start | bytes 393224 | tf_op jit(solution)/shard_map/ppermute | solution.py:40
  14.2 8.6 %collective-permute-start.7 = (bf16[16,4096]{1,0:T(8,128)(2,1)S(1)}, bf16[16,4096]{1,0:T(8,128)(2,1)S(1)}, u32[]{:S(2)}, u32[]{:S(2)}) collective-permute-start(bf16[16,4096]{1,0:T(8,128)(2,1)S(1)} %get-tuple-element.24), channel_id=1, source_target_pairs={{0,9},{1,8},{2,11},{3,10},{4,13},{5,12},{6,15},{7,14},{8,1},{9,0},... | collective-permute-start | bytes 393224 | tf_op jit(solution)/shard_map/ppermute | solution.py:40
  14.2 10.5 %collective-permute-start.3 = (bf16[16,4096]{1,0:T(8,128)(2,1)S(1)}, bf16[16,4096]{1,0:T(8,128)(2,1)S(1)}, u32[]{:S(2)}, u32[]{:S(2)}) collective-permute-start(bf16[16,4096]{1,0:T(8,128)(2,1)S(1)} %get-tuple-element.24), channel_id=1, source_target_pairs={{0,8},{1,9},{2,10},{3,11},{4,12},{5,13},{6,14},{7,15},{8,0},{9,1},... | collective-permute-start | bytes 393224 | tf_op jit(solution)/shard_map/ppermute | solution.py:40
  14.9 9.8 %collective-permute-start.8 = (bf16[16,4096]{1,0:T(8,128)(2,1)S(1)}, bf16[16,4096]{1,0:T(8,128)(2,1)S(1)}, u32[]{:S(2)}, u32[]{:S(2)}) collective-permute-start(bf16[16,4096]{1,0:T(8,128)(2,1)S(1)} %get-tuple-element.25), channel_id=1, source_target_pairs={{0,17},{1,16},{2,19},{3,18},{4,21},{5,20},{6,23},{7,22},{8,25},{9,... | collective-permute-start | bytes 393224 | tf_op jit(solution)/shard_map/ppermute | solution.py:40
  17.3 7.4 %collective-permute-start.4 = (bf16[16,4096]{1,0:T(8,128)(2,1)S(1)}, bf16[16,4096]{1,0:T(8,128)(2,1)S(1)}, u32[]{:S(2)}, u32[]{:S(2)}) collective-permute-start(bf16[16,4096]{1,0:T(8,128)(2,1)S(1)} %get-tuple-element.25), channel_id=1, source_target_pairs={{0,16},{1,17},{2,18},{3,19},{4,20},{5,21},{6,22},{7,23},{8,24},{9,... | collective-permute-start | bytes 393224 | tf_op jit(solution)/shard_map/ppermute | solution.py:40
  20.1 5.3 %collective-permute-start.9 = (bf16[16,4096]{1,0:T(8,128)(2,1)S(1)}, bf16[16,4096]{1,0:T(8,128)(2,1)S(1)}, u32[]{:S(2)}, u32[]{:S(2)}) collective-permute-start(bf16[16,4096]{1,0:T(8,128)(2,1)S(1)} %get-tuple-element.26), channel_id=1, source_target_pairs={{0,25},{1,24},{2,27},{3,26},{4,29},{5,28},{6,31},{7,30},{8,17},{9,... | collective-permute-start | bytes 393224 | tf_op jit(solution)/shard_map/ppermute | solution.py:40
  22.8 6.5 %collective-permute-start.5 = (bf16[16,4096]{1,0:T(8,128)(2,1)S(1)}, bf16[16,4096]{1,0:T(8,128)(2,1)S(1)}, u32[]{:S(2)}, u32[]{:S(2)}) collective-permute-start(bf16[16,4096]{1,0:T(8,128)(2,1)S(1)} %get-tuple-element.26), channel_id=1, source_target_pairs={{0,24},{1,25},{2,26},{3,27},{4,28},{5,29},{6,30},{7,31},{8,16},{9,... | collective-permute-start | bytes 393224 | tf_op jit(solution)/shard_map/ppermute | solution.py:40
  29.5 14.8 %copy-start = (bf16[4096,4]{0,1:T(4,128)(2,1)S(1)}, bf16[4096,4]{0,1:T(4,128)(2,1)}, u32[]{:S(2)}) copy-start(bf16[4096,4]{0,1:T(4,128)(2,1)} %param.7) | copy-start | bytes 98308
  37.6 3.8 %collective-permute-start.10 = (bf16[16,4096]{1,0:T(8,128)(2,1)S(1)}, bf16[16,4096]{1,0:T(8,128)(2,1)S(1)}, u32[]{:S(2)}, u32[]{:S(2)}) collective-permute-start(bf16[16,4096]{1,0:T(8,128)(2,1)S(1)} %get-tuple-element.28), channel_id=1, source_target_pairs={{0,8},{1,9},{2,10},{3,11},{4,12},{5,13},{6,14},{7,15},{8,0},{9,1},... | collective-permute-start | bytes 393224 | tf_op jit(solution)/shard_map/ppermute | solution.py:40
  37.8 6.4 %collective-permute-start.11 = (bf16[16,4096]{1,0:T(8,128)(2,1)S(1)}, bf16[16,4096]{1,0:T(8,128)(2,1)S(1)}, u32[]{:S(2)}, u32[]{:S(2)}) collective-permute-start(bf16[16,4096]{1,0:T(8,128)(2,1)S(1)} %get-tuple-element.29), channel_id=1, source_target_pairs={{0,16},{1,17},{2,18},{3,19},{4,20},{5,21},{6,22},{7,23},{8,24},{9,... | collective-permute-start | bytes 393224 | tf_op jit(solution)/shard_map/ppermute | solution.py:40
  39.6 6.7 %collective-permute-start.12 = (bf16[16,4096]{1,0:T(8,128)(2,1)S(1)}, bf16[16,4096]{1,0:T(8,128)(2,1)S(1)}, u32[]{:S(2)}, u32[]{:S(2)}) collective-permute-start(bf16[16,4096]{1,0:T(8,128)(2,1)S(1)} %get-tuple-element.30), channel_id=1, source_target_pairs={{0,24},{1,25},{2,26},{3,27},{4,28},{5,29},{6,30},{7,31},{8,16},{9,... | collective-permute-start | bytes 393224 | tf_op jit(solution)/shard_map/ppermute | solution.py:40
  39.6 6.7 %collective-permute-start.13 = (bf16[16,4096]{1,0:T(8,128)(2,1)S(1)}, bf16[16,4096]{1,0:T(8,128)(2,1)S(1)}, u32[]{:S(2)}, u32[]{:S(2)}) collective-permute-start(bf16[16,4096]{1,0:T(8,128)(2,1)S(1)} %get-tuple-element.31), channel_id=1, source_target_pairs={{0,1},{1,0},{2,3},{3,2},{4,5},{5,4},{6,7},{7,6},{8,9},{9,8},{10,11... | collective-permute-start | bytes 393224 | tf_op jit(solution)/shard_map/ppermute | solution.py:40
  40.1 13.1 %collective-permute-start.14 = (bf16[16,4096]{1,0:T(8,128)(2,1)S(1)}, bf16[16,4096]{1,0:T(8,128)(2,1)S(1)}, u32[]{:S(2)}, u32[]{:S(2)}) collective-permute-start(bf16[16,4096]{1,0:T(8,128)(2,1)S(1)} %get-tuple-element.32), channel_id=1, source_target_pairs={{0,9},{1,8},{2,11},{3,10},{4,13},{5,12},{6,15},{7,14},{8,1},{9,0},... | collective-permute-start | bytes 393224 | tf_op jit(solution)/shard_map/ppermute | solution.py:40
  41.3 11.9 %collective-permute-start.15 = (bf16[16,4096]{1,0:T(8,128)(2,1)S(1)}, bf16[16,4096]{1,0:T(8,128)(2,1)S(1)}, u32[]{:S(2)}, u32[]{:S(2)}) collective-permute-start(bf16[16,4096]{1,0:T(8,128)(2,1)S(1)} %get-tuple-element.33), channel_id=1, source_target_pairs={{0,17},{1,16},{2,19},{3,18},{4,21},{5,20},{6,23},{7,22},{8,25},{9,... | collective-permute-start | bytes 393224 | tf_op jit(solution)/shard_map/ppermute | solution.py:40
  44.2 9.0 %collective-permute-start.16 = (bf16[16,4096]{1,0:T(8,128)(2,1)S(1)}, bf16[16,4096]{1,0:T(8,128)(2,1)S(1)}, u32[]{:S(2)}, u32[]{:S(2)}) collective-permute-start(bf16[16,4096]{1,0:T(8,128)(2,1)S(1)} %get-tuple-element.34), channel_id=1, source_target_pairs={{0,25},{1,24},{2,27},{3,26},{4,29},{5,28},{6,31},{7,30},{8,17},{9,... | collective-permute-start | bytes 393224 | tf_op jit(solution)/shard_map/ppermute | solution.py:40
  53.6 4.5 %collective-permute-start.17 = (bf16[8,4096]{1,0:T(8,128)(2,1)S(1)}, bf16[8,4096]{1,0:T(8,128)(2,1)S(1)}, u32[]{:S(2)}, u32[]{:S(2)}) collective-permute-start(bf16[8,4096]{1,0:T(8,128)(2,1)S(1)} %get-tuple-element.38), channel_id=1, source_target_pairs={{0,2},{1,3},{2,0},{3,1},{4,6},{5,7},{6,4},{7,5},{8,10},{9,11},{10,... | collective-permute-start | bytes 196616 | tf_op jit(solution)/shard_map/ppermute | solution.py:40
  54.7 8.5 %collective-permute-start.18 = (bf16[8,4096]{1,0:T(8,128)(2,1)S(1)}, bf16[8,4096]{1,0:T(8,128)(2,1)S(1)}, u32[]{:S(2)}, u32[]{:S(2)}) collective-permute-start(bf16[8,4096]{1,0:T(8,128)(2,1)S(1)} %get-tuple-element.39), channel_id=1, source_target_pairs={{0,4},{1,5},{2,6},{3,7},{4,0},{5,1},{6,2},{7,3},{8,12},{9,13},{10,... | collective-permute-start | bytes 196616 | tf_op jit(solution)/shard_map/ppermute | solution.py:40
  57.0 6.3 %collective-permute-start.19 = (bf16[8,4096]{1,0:T(8,128)(2,1)S(1)}, bf16[8,4096]{1,0:T(8,128)(2,1)S(1)}, u32[]{:S(2)}, u32[]{:S(2)}) collective-permute-start(bf16[8,4096]{1,0:T(8,128)(2,1)S(1)} %get-tuple-element.40), channel_id=1, source_target_pairs={{0,6},{1,7},{2,4},{3,5},{4,2},{5,3},{6,0},{7,1},{8,14},{9,15},{10,... | collective-permute-start | bytes 196616 | tf_op jit(solution)/shard_map/ppermute | solution.py:40
where the time goes:
time: 64 us; the launch traced here: 63.9 us
  waiting for transfers between devices  29.7 us (46%)
  starting transfers between devices  22.8 us (36%)
  Pallas kernels  11.1 us (17%)
    ppermute x20, waiting for transfers between devices, swap(): return lax.ppermute(value, ('expert', 'shard'), pairs)  29.7 us
    ppermute x20, starting transfers between devices, swap(): return lax.ppermute(value, ('expert', 'shard'), pairs)  22.8 us
    pallas_call x1, Pallas kernels, shards_program(): pl.pallas_call(functools.partial(ffn_kernel, parts, tile_width, OUT_TILE)...  8.06 us
  transfers between devices with their start and end apart: 20, of which 11 were waited for; matrix products, arithmetic and copies ran while one was open for 0% of the time, Pallas kernels for 1%

commit v1 on v0

--- a/solution.py
+++ b/solution.py
@@ -11,7 +11,7 @@
 LANES = 128
 HIDDEN_TILE = 256
 OUT_TILE = 1024
-LONG = 2e10
+LONG = 6e10
 MIB = 1 << 20
 
 
@@ -125,14 +125,17 @@
     low_ref[...] = (weights - high.astype(jnp.float32)).astype(jnp.bfloat16)
 
 
-def ffn_kernel(parts, tile_width, out_tile, *refs):
-    row_refs = refs[:parts]
-    gate_ref, up_ref, down_ref = refs[parts : parts + 3]
-    out_refs = refs[parts + 3 : 2 * parts + 3]
-    rows, hidden = refs[2 * parts + 3 :]
-    per_part = row_refs[0].shape[0]
+def ffn_kernel(parts, halves, tile_width, out_tile, *refs):
+    pieces = parts * halves
+    row_refs = refs[:pieces]
+    gate_ref, up_ref, down_ref = refs[pieces : pieces + 3]
+    out_refs = refs[pieces + 3 : 2 * pieces + 3]
+    rows, hidden = refs[2 * pieces + 3 :]
+    per_piece = row_refs[0].shape[0]
+    per_part = per_piece * halves
     for part in range(parts):
-        rows[pl.ds(part * per_part, per_part), :] = row_refs[part][...]
+        mine = row_refs[part * halves : (part + 1) * halves]
+        rows[pl.ds(part * per_part, per_part), :] = gather_blocks(mine)
 
     @pl.loop(0, hidden.shape[1] // tile_width)
     def _(tile):
@@ -144,17 +147,17 @@
     @pl.loop(0, down_ref.shape[1] // out_tile)
     def _(tile):
         columns = pl.ds(pl.multiple_of(tile * out_tile, out_tile), out_tile)
-        result = dot(hidden[...], down_ref[:, columns]).astype(jnp.bfloat16)
-        for part in range(parts):
-            out_refs[part][:, columns] = result[part * per_part : (part + 1) * per_part]
+        result = dot(hidden[...], down_ref[:, columns])
+        for piece in range(pieces):
+            mine = result[piece * per_piece : (piece + 1) * per_piece]
+            out_refs[piece][:, columns] = mine.astype(jnp.bfloat16)
 
 
 def combine_kernel(parts, n_experts, blocks, *refs):
-    part_refs = refs[:parts]
     high_ref, low_ref = refs[parts : parts + 2]
     out_refs = refs[parts + 2 :]
     inner = parts // n_experts
-    rows = jnp.concatenate([ref[...] for ref in part_refs], axis=0)
+    rows = gather_blocks(refs[:parts])
     high = jnp.concatenate([high_ref[...]] * inner, axis=0)
     low = jnp.concatenate([low_ref[...]] * inner, axis=0)
     mixed = dot(high, rows, (0, 0)) + dot(low, rows, (0, 0))
@@ -180,7 +183,6 @@
     per_expert = outer * slots_per
     parts = inner * n_experts
     n_rows = parts * per_expert
-    gathered = outer * local_tokens
     n_hidden = w_gate.shape[2]
     bf16 = jnp.bfloat16
     vmem = pl.BlockSpec(memory_space=pltpu.VMEM)
@@ -202,53 +204,67 @@
     along = [packed] + [exchange(packed, 0, d * inner) for d in range(1, outer)]
 
     tile_width = HIDDEN_TILE if n_hidden % HIDDEN_TILE == 0 else LANES
-    buffers = pl.pallas_call(
-        functools.partial(dispatch_kernel, outer, n_experts, width),
-        name="dispatch",
-        out_shape=[jax.ShapeDtypeStruct((per_expert, width), bf16)] * n_experts,
-        in_specs=[vmem] * outer,
-        out_specs=[vmem] * n_experts,
-        compiler_params=pltpu.CompilerParams(vmem_limit_bytes=6 * MIB),
-        cost_estimate=cost(LONG, 4 * MIB),
-    )(*along)
-
+    halves = 2
+    per_half = outer // halves
+    piece_rows = per_half * slots_per
     order = [(i, k) for i in range(inner) for k in range(n_experts)]
-    row_parts = [buffers[k] if (i, k) == (0, 0) else exchange(buffers[k], k, i) for i, k in order]
-
-    high, low = pl.pallas_call(
-        functools.partial(gates_kernel, outer, n_experts, width),
-        name="gates",
-        out_shape=[jax.ShapeDtypeStruct((n_experts * per_expert, gathered), bf16)] * 2,
-        in_specs=[vmem] * (outer + 1),
-        out_specs=[vmem] * 2,
-        compiler_params=pltpu.CompilerParams(vmem_limit_bytes=6 * MIB),
-        cost_estimate=cost(LONG, MIB),
-    )(*along, router.T)
-
-    out_parts = pl.pallas_call(
-        functools.partial(ffn_kernel, parts, tile_width, OUT_TILE),
+
+    def dispatch(half):
+        return pl.pallas_call(
+            functools.partial(dispatch_kernel, per_half, n_experts, width),
+            out_shape=[jax.ShapeDtypeStruct((piece_rows, width), bf16)] * n_experts,
+            in_specs=[vmem] * per_half,
+            out_specs=[vmem] * n_experts,
+            compiler_params=pltpu.CompilerParams(vmem_limit_bytes=6 * MIB),
+            cost_estimate=cost(4e8, 4 * MIB),
+        )(*along[half * per_half : (half + 1) * per_half])
+
+    def weights(half):
+        n_tokens = per_half * local_tokens
+        return pl.pallas_call(
+            functools.partial(gates_kernel, per_half, n_experts, width),
+            out_shape=[jax.ShapeDtypeStruct((n_experts * piece_rows, n_tokens), bf16)] * 2,
+            in_specs=[vmem] * (per_half + 1),
+            out_specs=[vmem] * 2,
+            compiler_params=pltpu.CompilerParams(vmem_limit_bytes=6 * MIB),
+            cost_estimate=cost(4e8, MIB),
+        )(*along[half * per_half : (half + 1) * per_half], router.T)
+
+    arrived = []
+    for half in range(halves):
+        buffers = dispatch(half)
+        arrived.append(
+            [buffers[k] if (i, k) == (0, 0) else exchange(buffers[k], k, i) for i, k in order]
+        )
+    combine_weights = [weights(half) for half in range(halves)]
+
+    pieces = parts * halves
+    sent = pl.pallas_call(
+        functools.partial(ffn_kernel, parts, halves, tile_width, OUT_TILE),
         name="ffn",
-        out_shape=[jax.ShapeDtypeStruct((per_expert, width), bf16)] * parts,
-        in_specs=[vmem] * (parts + 3),
-        out_specs=[vmem] * parts,
+        out_shape=[jax.ShapeDtypeStruct((piece_rows, width), bf16)] * pieces,
+        in_specs=[vmem] * (pieces + 3),
+        out_specs=[vmem] * pieces,
         scratch_shapes=[pltpu.VMEM((n_rows, width), bf16), pltpu.VMEM((n_rows, n_hidden), bf16)],
         compiler_params=pltpu.CompilerParams(vmem_limit_bytes=5 * MIB),
         cost_estimate=cost(6 * n_rows * width * n_hidden, 6 * width * n_hidden),
-    )(*row_parts, w_gate, w_up, w_down)
-
-    back = [
-        out_parts[j] if (i, k) == (0, 0) else exchange(out_parts[j], k, i)
-        for j, (i, k) in enumerate(order)
-    ]
-    mixed = pl.pallas_call(
-        functools.partial(combine_kernel, parts, n_experts, outer),
-        name="combine",
-        out_shape=[jax.ShapeDtypeStruct((local_tokens, width), bf16)] * outer,
-        in_specs=[vmem] * (parts + 2),
-        out_specs=[vmem] * outer,
-        compiler_params=pltpu.CompilerParams(vmem_limit_bytes=20 * MIB),
-        cost_estimate=cost(4 * n_rows * gathered * width, 4 * MIB),
-    )(*back, high, low)
+    )(*(arrived[half][j] for j in range(parts) for half in range(halves)), w_gate, w_up, w_down)
+
+    mixed = []
+    for half in range(halves):
+        mine = sent[half::halves]
+        back = [
+            mine[j] if (i, k) == (0, 0) else exchange(mine[j], k, i)
+            for j, (i, k) in enumerate(order)
+        ]
+        mixed += pl.pallas_call(
+            functools.partial(combine_kernel, parts, n_experts, per_half),
+            out_shape=[jax.ShapeDtypeStruct((local_tokens, width), bf16)] * per_half,
+            in_specs=[vmem] * (parts + 2),
+            out_specs=[vmem] * per_half,
+            compiler_params=pltpu.CompilerParams(vmem_limit_bytes=20 * MIB),
+            cost_estimate=cost(4e8, 4 * MIB),
+        )(*back, *combine_weights[half])
     home = [mixed[0]] + [exchange(mixed[d], 0, d * inner) for d in range(1, outer)]
     return pl.pallas_call(
         final_kernel,

time: 64 us -> 66.2 us (1.034)
  starting transfers between devices: 22.8 us -> 40 us
  waiting for transfers between devices: 29.7 us -> 13.8 us
  Pallas kernels: 11.1 us -> 12.2 us
    ppermute x20 -> x34, starting transfers between devices: 22.8 us -> 40 us  [swap(): return lax.ppermute(value, ('expert', 'shard'), pairs)]
    ppermute x20 -> x34, waiting for transfers between devices: 29.7 us -> 13.8 us  [swap(): return lax.ppermute(value, ('expert', 'shard'), pairs)]
    pallas_call x4 -> x7, Pallas kernels: 9.34 us -> 10.4 us  [the longest x1 8.31 us: shards_program(): pl.pallas_call(functools.partial(ffn_kernel, parts, halves, tile_width, O...]
  transfers between devices with their start and end apart: 20 -> 34, of which waited for: 11 -> 11; matrix products, arithmetic and copies ran while one was open for 0% -> 0% of each run, Pallas kernels for 1% -> 3%
where the time goes in v1:
time: 66.2 us; the launch traced here: 66.1 us
  starting transfers between devices  40 us (60%)
  waiting for transfers between devices  13.8 us (21%)
  Pallas kernels  12.2 us (18%)
    ppermute x34, starting transfers between devices, swap(): return lax.ppermute(value, ('expert', 'shard'), pairs)  40 us
    ppermute x34, waiting for transfers between devices, swap(): return lax.ppermute(value, ('expert', 'shard'), pairs)  13.8 us
    pallas_call x1, Pallas kernels, shards_program(): pl.pallas_call(functools.partial(ffn_kernel, parts, halves, tile_width, O...  8.31 us
  transfers between devices with their start and end apart: 34, of which 11 were waited for; matrix products, arithmetic and copies ran while one was open for 0% of the time, Pallas kernels for 3%

profile of v1, /device:TPU:0, one launch (start us, length us, event | category | flops | bytes accessed | tf_op | source)
XLA Modules:
  0.0 66.1 jit_solution(3713987306753422527)
XLA Ops:
  0.0 1.1 %pack.1.refs_0_ = bf16[8,4224]{1,0:T(8,128)(2,1)S(1)} custom-call(bf16[8,4096]{1,0:T(8,128)(2,1)} %tokens_ref.1, s32[2,8]{1,0:T(2,128)} %bitcast.10), custom_call_target="tpu_custom_call" | custom-call | flops 60000002048 | bytes 1048576 | tf_op jit(solution)/shard_map/pack/pallas_call | solution.py:195
  1.1 3.1 %collective-permute-start = (bf16[8,4224]{1,0:T(8,128)(2,1)S(1)}, bf16[8,4224]{1,0:T(8,128)(2,1)S(1)}, u32[]{:S(2)}, u32[]{:S(2)}) collective-permute-start(bf16[8,4224]{1,0:T(8,128)(2,1)S(1)} %pack.1.refs_0_), channel_id=1, source_target_pairs={{0,2},{1,3},{2,0},{3,1},{4,6},{5,7},{6,4},{7,5},{8,10},{9,11},{10,... | collective-permute-start | bytes 202760 | tf_op jit(solution)/shard_map/ppermute | solution.py:40
  4.2 2.5 %collective-permute-start.2 = (bf16[8,4224]{1,0:T(8,128)(2,1)S(1)}, bf16[8,4224]{1,0:T(8,128)(2,1)S(1)}, u32[]{:S(2)}, u32[]{:S(2)}) collective-permute-start(bf16[8,4224]{1,0:T(8,128)(2,1)S(1)} %pack.1.refs_0_), channel_id=1, source_target_pairs={{0,6},{1,7},{2,4},{3,5},{4,2},{5,3},{6,0},{7,1},{8,14},{9,15},{10,... | collective-permute-start | bytes 202760 | tf_op jit(solution)/shard_map/ppermute | solution.py:40
  6.8 0.4 shard_map.64
  7.2 1.7 %collective-permute-start.9 = (bf16[8,4096]{1,0:T(8,128)(2,1)S(1)}, bf16[8,4096]{1,0:T(8,128)(2,1)S(1)}, u32[]{:S(2)}, u32[]{:S(2)}) collective-permute-start(bf16[8,4096]{1,0:T(8,128)(2,1)S(1)} %get-tuple-element.37.refs_0_), channel_id=1, source_target_pairs={{0,1},{1,0},{2,3},{3,2},{4,5},{5,4},{6,7},{7,6},{8,9},{9,8},{10,11... | collective-permute-start | bytes 196616 | tf_op jit(solution)/shard_map/ppermute | solution.py:40
  8.9 0.5 collective-permute-start.3
  9.5 1.7 %collective-permute-done.2.refs_1_ = bf16[8,4224]{1,0:T(8,128)(2,1)S(1)} collective-permute-done((bf16[8,4224]{1,0:T(8,128)(2,1)S(1)}, bf16[8,4224]{1,0:T(8,128)(2,1)S(1)}, u32[]{:S(2)}, u32[]{:S(2)}) %collective-permute-start.2) | collective-permute-done | bytes 67616 | tf_op jit(solution)/shard_map/ppermute | solution.py:40
  11.2 2.4 %collective-permute-start.13 = (bf16[8,4096]{1,0:T(8,128)(2,1)S(1)}, bf16[8,4096]{1,0:T(8,128)(2,1)S(1)}, u32[]{:S(2)}, u32[]{:S(2)}) collective-permute-start(bf16[8,4096]{1,0:T(8,128)(2,1)S(1)} %get-tuple-element.41), channel_id=1, source_target_pairs={{0,17},{1,16},{2,19},{3,18},{4,21},{5,20},{6,23},{7,22},{8,25},{9,... | collective-permute-start | bytes 196616 | tf_op jit(solution)/shard_map/ppermute | solution.py:40
  13.6 1.2 %collective-permute-start.5 = (bf16[8,4096]{1,0:T(8,128)(2,1)S(1)}, bf16[8,4096]{1,0:T(8,128)(2,1)S(1)}, u32[]{:S(2)}, u32[]{:S(2)}) collective-permute-start(bf16[8,4096]{1,0:T(8,128)(2,1)S(1)} %get-tuple-element.41), channel_id=1, source_target_pairs={{0,16},{1,17},{2,18},{3,19},{4,20},{5,21},{6,22},{7,23},{8,24},{9,... | collective-permute-start | bytes 196616 | tf_op jit(solution)/shard_map/ppermute | solution.py:40
  14.8 0.4 shard_map.65
  15.2 0.8 %collective-permute-start.15 = (bf16[8,4096]{1,0:T(8,128)(2,1)S(1)}, bf16[8,4096]{1,0:T(8,128)(2,1)S(1)}, u32[]{:S(2)}, u32[]{:S(2)}) collective-permute-start(bf16[8,4096]{1,0:T(8,128)(2,1)S(1)} %get-tuple-element.43), channel_id=1, source_target_pairs={{0,25},{1,24},{2,27},{3,26},{4,29},{5,28},{6,31},{7,30},{8,17},{9,... | collective-permute-start | bytes 196616 | tf_op jit(solution)/shard_map/ppermute | solution.py:40
  16.1 1.9 %collective-permute-start.7 = (bf16[8,4096]{1,0:T(8,128)(2,1)S(1)}, bf16[8,4096]{1,0:T(8,128)(2,1)S(1)}, u32[]{:S(2)}, u32[]{:S(2)}) collective-permute-start(bf16[8,4096]{1,0:T(8,128)(2,1)S(1)} %get-tuple-element.43), channel_id=1, source_target_pairs={{0,24},{1,25},{2,26},{3,27},{4,28},{5,29},{6,30},{7,31},{8,16},{9,... | collective-permute-start | bytes 196616 | tf_op jit(solution)/shard_map/ppermute | solution.py:40
  18.0 0.5 collective-permute-start.10
  18.5 0.5 collective-permute-start.12
  19.0 1.1 %collective-permute-start.4 = (bf16[8,4096]{1,0:T(8,128)(2,1)S(1)}, bf16[8,4096]{1,0:T(8,128)(2,1)S(1)}, u32[]{:S(2)}, u32[]{:S(2)}) collective-permute-start(bf16[8,4096]{1,0:T(8,128)(2,1)S(1)} %get-tuple-element.40), channel_id=1, source_target_pairs={{0,8},{1,9},{2,10},{3,11},{4,12},{5,13},{6,14},{7,15},{8,0},{9,1},... | collective-permute-start | bytes 196616 | tf_op jit(solution)/shard_map/ppermute | solution.py:40
  20.1 0.4 collective-permute-done.15.refs_14_
  20.5 1.5 %collective-permute-start.14 = (bf16[8,4096]{1,0:T(8,128)(2,1)S(1)}, bf16[8,4096]{1,0:T(8,128)(2,1)S(1)}, u32[]{:S(2)}, u32[]{:S(2)}) collective-permute-start(bf16[8,4096]{1,0:T(8,128)(2,1)S(1)} %get-tuple-element.42), channel_id=1, source_target_pairs={{0,17},{1,16},{2,19},{3,18},{4,21},{5,20},{6,23},{7,22},{8,25},{9,... | collective-permute-start | bytes 196616 | tf_op jit(solution)/shard_map/ppermute | solution.py:40
  22.0 1.5 %collective-permute-start.6 = (bf16[8,4096]{1,0:T(8,128)(2,1)S(1)}, bf16[8,4096]{1,0:T(8,128)(2,1)S(1)}, u32[]{:S(2)}, u32[]{:S(2)}) collective-permute-start(bf16[8,4096]{1,0:T(8,128)(2,1)S(1)} %get-tuple-element.42), channel_id=1, source_target_pairs={{0,16},{1,17},{2,18},{3,19},{4,20},{5,21},{6,22},{7,23},{8,24},{9,... | collective-permute-start | bytes 196616 | tf_op jit(solution)/shard_map/ppermute | solution.py:40
  23.6 1.6 %collective-permute-start.8 = (bf16[8,4096]{1,0:T(8,128)(2,1)S(1)}, bf16[8,4096]{1,0:T(8,128)(2,1)S(1)}, u32[]{:S(2)}, u32[]{:S(2)}) collective-permute-start(bf16[8,4096]{1,0:T(8,128)(2,1)S(1)} %get-tuple-element.44), channel_id=1, source_target_pairs={{0,24},{1,25},{2,26},{3,27},{4,28},{5,29},{6,30},{7,31},{8,16},{9,... | collective-permute-start | bytes 196616 | tf_op jit(solution)/shard_map/ppermute | solution.py:40
  25.2 0.9 %collective-permute-done.14.refs_13_ = bf16[8,4096]{1,0:T(8,128)(2,1)S(1)} collective-permute-done((bf16[8,4096]{1,0:T(8,128)(2,1)S(1)}, bf16[8,4096]{1,0:T(8,128)(2,1)S(1)}, u32[]{:S(2)}, u32[]{:S(2)}) %collective-permute-start.14) | collective-permute-done | bytes 65568 | tf_op jit(solution)/shard_map/ppermute | solution.py:40
  26.1 0.9 %collective-permute-done.6.refs_5_ = bf16[8,4096]{1,0:T(8,128)(2,1)S(1)} collective-permute-done((bf16[8,4096]{1,0:T(8,128)(2,1)S(1)}, bf16[8,4096]{1,0:T(8,128)(2,1)S(1)}, u32[]{:S(2)}, u32[]{:S(2)}) %collective-permute-start.6) | collective-permute-done | bytes 65568 | tf_op jit(solution)/shard_map/ppermute | solution.py:40
  27.0 1.3 %collective-permute-done.16.refs_15_ = bf16[8,4096]{1,0:T(8,128)(2,1)S(1)} collective-permute-done((bf16[8,4096]{1,0:T(8,128)(2,1)S(1)}, bf16[8,4096]{1,0:T(8,128)(2,1)S(1)}, u32[]{:S(2)}, u32[]{:S(2)}) %collective-permute-start.16) | collective-permute-done | bytes 65568 | tf_op jit(solution)/shard_map/ppermute | solution.py:40
  28.3 0.9 %collective-permute-done.8.refs_7_ = bf16[8,4096]{1,0:T(8,128)(2,1)S(1)} collective-permute-done((bf16[8,4096]{1,0:T(8,128)(2,1)S(1)}, bf16[8,4096]{1,0:T(8,128)(2,1)S(1)}, u32[]{:S(2)}, u32[]{:S(2)}) %collective-permute-start.8) | collective-permute-done | bytes 65568 | tf_op jit(solution)/shard_map/ppermute | solution.py:40
  29.3 8.3 %ffn.1 = (bf16[8,4096]{1,0:T(8,128)(2,1)S(1)}, bf16[8,4096]{1,0:T(8,128)(2,1)S(1)}, bf16[8,4096]{1,0:T(8,128)(2,1)S(1)}, bf16[8,4096]{1,0:T(8,128)(2,1)S(1)}, bf...) custom-call(bf16[8,4096]{1,0:T(8,128)(2,1)S(1)} %get-tuple-element.3, ...), custom_call_target="tpu_custom_call" | custom-call | flops 5637144576 | bytes 44040192 | tf_op jit(solution)/shard_map/ffn/pallas_call | solution.py:242
  37.8 1.1 %collective-permute-start.18 = (bf16[8,4096]{1,0:T(8,128)(2,1)S(1)}, bf16[8,4096]{1,0:T(8,128)(2,1)S(1)}, u32[]{:S(2)}, u32[]{:S(2)}) collective-permute-start(bf16[8,4096]{1,0:T(8,128)(2,1)S(1)} %get-tuple-element.47), channel_id=1, source_target_pairs={{0,16},{1,17},{2,18},{3,19},{4,20},{5,21},{6,22},{7,23},{8,24},{9,... | collective-permute-start | bytes 196616 | tf_op jit(solution)/shard_map/ppermute | solution.py:40
  38.9 0.7 %collective-permute-start.19 = (bf16[8,4096]{1,0:T(8,128)(2,1)S(1)}, bf16[8,4096]{1,0:T(8,128)(2,1)S(1)}, u32[]{:S(2)}, u32[]{:S(2)}) collective-permute-start(bf16[8,4096]{1,0:T(8,128)(2,1)S(1)} %get-tuple-element.48), channel_id=1, source_target_pairs={{0,24},{1,25},{2,26},{3,27},{4,28},{5,29},{6,30},{7,31},{8,16},{9,... | collective-permute-start | bytes 196616 | tf_op jit(solution)/shard_map/ppermute | solution.py:40
  39.5 1.0 %collective-permute-start.20 = (bf16[8,4096]{1,0:T(8,128)(2,1)S(1)}, bf16[8,4096]{1,0:T(8,128)(2,1)S(1)}, u32[]{:S(2)}, u32[]{:S(2)}) collective-permute-start(bf16[8,4096]{1,0:T(8,128)(2,1)S(1)} %get-tuple-element.49), channel_id=1, source_target_pairs={{0,1},{1,0},{2,3},{3,2},{4,5},{5,4},{6,7},{7,6},{8,9},{9,8},{10,11... | collective-permute-start | bytes 196616 | tf_op jit(solution)/shard_map/ppermute | solution.py:40
  40.5 0.7 %collective-permute-start.21 = (bf16[8,4096]{1,0:T(8,128)(2,1)S(1)}, bf16[8,4096]{1,0:T(8,128)(2,1)S(1)}, u32[]{:S(2)}, u32[]{:S(2)}) collective-permute-start(bf16[8,4096]{1,0:T(8,128)(2,1)S(1)} %get-tuple-element.50), channel_id=1, source_target_pairs={{0,9},{1,8},{2,11},{3,10},{4,13},{5,12},{6,15},{7,14},{8,1},{9,0},... | collective-permute-start | bytes 196616 | tf_op jit(solution)/shard_map/ppermute | solution.py:40
  41.3 1.0 %collective-permute-start.22 = (bf16[8,4096]{1,0:T(8,128)(2,1)S(1)}, bf16[8,4096]{1,0:T(8,128)(2,1)S(1)}, u32[]{:S(2)}, u32[]{:S(2)}) collective-permute-start(bf16[8,4096]{1,0:T(8,128)(2,1)S(1)} %get-tuple-element.51), channel_id=1, source_target_pairs={{0,17},{1,16},{2,19},{3,18},{4,21},{5,20},{6,23},{7,22},{8,25},{9,... | collective-permute-start | bytes 196616 | tf_op jit(solution)/shard_map/ppermute | solution.py:40
  42.5 1.4 %collective-permute-start.23 = (bf16[8,4096]{1,0:T(8,128)(2,1)S(1)}, bf16[8,4096]{1,0:T(8,128)(2,1)S(1)}, u32[]{:S(2)}, u32[]{:S(2)}) collective-permute-start(bf16[8,4096]{1,0:T(8,128)(2,1)S(1)} %get-tuple-element.52), channel_id=1, source_target_pairs={{0,25},{1,24},{2,27},{3,26},{4,29},{5,28},{6,31},{7,30},{8,17},{9,... | collective-permute-start | bytes 196616 | tf_op jit(solution)/shard_map/ppermute | solution.py:40
  43.9 0.4 collective-permute-start.25
  44.4 1.1 %collective-permute-start.26 = (bf16[8,4096]{1,0:T(8,128)(2,1)S(1)}, bf16[8,4096]{1,0:T(8,128)(2,1)S(1)}, u32[]{:S(2)}, u32[]{:S(2)}) collective-permute-start(bf16[8,4096]{1,0:T(8,128)(2,1)S(1)} %get-tuple-element.59), channel_id=1, source_target_pairs={{0,16},{1,17},{2,18},{3,19},{4,20},{5,21},{6,22},{7,23},{8,24},{9,... | collective-permute-start | bytes 196616 | tf_op jit(solution)/shard_map/ppermute | solution.py:40
  45.4 0.3 shard_map.68
  45.7 3.0 %collective-permute-start.27 = (bf16[8,4096]{1,0:T(8,128)(2,1)S(1)}, bf16[8,4096]{1,0:T(8,128)(2,1)S(1)}, u32[]{:S(2)}, u32[]{:S(2)}) collective-permute-start(bf16[8,4096]{1,0:T(8,128)(2,1)S(1)} %get-tuple-element.60), channel_id=1, source_target_pairs={{0,24},{1,25},{2,26},{3,27},{4,28},{5,29},{6,30},{7,31},{8,16},{9,... | collective-permute-start | bytes 196616 | tf_op jit(solution)/shard_map/ppermute | solution.py:40
  48.8 0.7 %collective-permute-start.29 = (bf16[8,4096]{1,0:T(8,128)(2,1)S(1)}, bf16[8,4096]{1,0:T(8,128)(2,1)S(1)}, u32[]{:S(2)}, u32[]{:S(2)}) collective-permute-start(bf16[8,4096]{1,0:T(8,128)(2,1)S(1)} %get-tuple-element.62), channel_id=1, source_target_pairs={{0,9},{1,8},{2,11},{3,10},{4,13},{5,12},{6,15},{7,14},{8,1},{9,0},... | collective-permute-start | bytes 196616 | tf_op jit(solution)/shard_map/ppermute | solution.py:40
  49.5 1.8 %collective-permute-start.30 = (bf16[8,4096]{1,0:T(8,128)(2,1)S(1)}, bf16[8,4096]{1,0:T(8,128)(2,1)S(1)}, u32[]{:S(2)}, u32[]{:S(2)}) collective-permute-start(bf16[8,4096]{1,0:T(8,128)(2,1)S(1)} %get-tuple-element.63), channel_id=1, source_target_pairs={{0,17},{1,16},{2,19},{3,18},{4,21},{5,20},{6,23},{7,22},{8,25},{9,... | collective-permute-start | bytes 196616 | tf_op jit(solution)/shard_map/ppermute | solution.py:40
  51.4 1.8 %collective-permute-start.31 = (bf16[8,4096]{1,0:T(8,128)(2,1)S(1)}, bf16[8,4096]{1,0:T(8,128)(2,1)S(1)}, u32[]{:S(2)}, u32[]{:S(2)}) collective-permute-start(bf16[8,4096]{1,0:T(8,128)(2,1)S(1)} %get-tuple-element.64), channel_id=1, source_target_pairs={{0,25},{1,24},{2,27},{3,26},{4,29},{5,28},{6,31},{7,30},{8,17},{9,... | collective-permute-start | bytes 196616 | tf_op jit(solution)/shard_map/ppermute | solution.py:40
  53.2 0.3 shard_map.66
  53.5 0.3 shard_map.67
  53.8 0.7 %collective-permute-start.24 = (bf16[8,4096]{1,0:T(8,128)(2,1)S(1)}, bf16[8,4096]{1,0:T(8,128)(2,1)S(1)}, u32[]{:S(2)}, u32[]{:S(2)}) collective-permute-start(bf16[8,4096]{1,0:T(8,128)(2,1)S(1)} %get-tuple-element.56), channel_id=1, source_target_pairs={{0,2},{1,3},{2,0},{3,1},{4,6},{5,7},{6,4},{7,5},{8,10},{9,11},{10,... | collective-permute-start | bytes 196616 | tf_op jit(solution)/shard_map/ppermute | solution.py:40
  54.5 0.5 collective-permute-done.30.refs_6_
  55.0 1.8 %collective-permute-done.31.refs_7_ = bf16[8,4096]{1,0:T(8,128)(2,1)S(1)} collective-permute-done((bf16[8,4096]{1,0:T(8,128)(2,1)S(1)}, bf16[8,4096]{1,0:T(8,128)(2,1)S(1)}, u32[]{:S(2)}, u32[]{:S(2)}) %collective-permute-start.31) | collective-permute-done | bytes 65568 | tf_op jit(solution)/shard_map/ppermute | solution.py:40
  56.8 0.3 shard_map.69
  57.1 2.2 %collective-permute-start.32 = (bf16[8,4096]{1,0:T(8,128)(2,1)S(1)}, bf16[8,4096]{1,0:T(8,128)(2,1)S(1)}, u32[]{:S(2)}, u32[]{:S(2)}) collective-permute-start(bf16[8,4096]{1,0:T(8,128)(2,1)S(1)} %get-tuple-element.67), channel_id=1, source_target_pairs={{0,4},{1,5},{2,6},{3,7},{4,0},{5,1},{6,2},{7,3},{8,12},{9,13},{10,... | collective-permute-start | bytes 196616 | tf_op jit(solution)/shard_map/ppermute | solution.py:40
  59.4 0.9 %collective-permute-start.33 = (bf16[8,4096]{1,0:T(8,128)(2,1)S(1)}, bf16[8,4096]{1,0:T(8,128)(2,1)S(1)}, u32[]{:S(2)}, u32[]{:S(2)}) collective-permute-start(bf16[8,4096]{1,0:T(8,128)(2,1)S(1)} %get-tuple-element.68), channel_id=1, source_target_pairs={{0,6},{1,7},{2,4},{3,5},{4,2},{5,3},{6,0},{7,1},{8,14},{9,15},{10,... | collective-permute-start | bytes 196616 | tf_op jit(solution)/shard_map/ppermute | solution.py:40
  60.2 4.4 %collective-permute-done.32.refs_2_ = bf16[8,4096]{1,0:T(8,128)(2,1)S(1)} collective-permute-done((bf16[8,4096]{1,0:T(8,128)(2,1)S(1)}, bf16[8,4096]{1,0:T(8,128)(2,1)S(1)}, u32[]{:S(2)}, u32[]{:S(2)}) %collective-permute-start.32) | collective-permute-done | bytes 65568 | tf_op jit(solution)/shard_map/ppermute | solution.py:40
  64.6 0.8 %collective-permute-done.33.refs_3_ = bf16[8,4096]{1,0:T(8,128)(2,1)S(1)} collective-permute-done((bf16[8,4096]{1,0:T(8,128)(2,1)S(1)}, bf16[8,4096]{1,0:T(8,128)(2,1)S(1)}, u32[]{:S(2)}, u32[]{:S(2)}) %collective-permute-start.33) | collective-permute-done | bytes 65568 | tf_op jit(solution)/shard_map/ppermute | solution.py:40
  65.4 0.7 %final.1 = bf16[8,4096]{1,0:T(8,128)(2,1)} custom-call(bf16[8,4096]{1,0:T(8,128)(2,1)S(1)} %get-tuple-element.55.refs_0_, bf16[8,4096]{1,0:T(8,128)(2,1)S(1)} %collective-permute-done.24.refs_1_, bf16[8,4096]{1,0:T(8,128)(2,1)S(1)} %collective-permute-done.32.refs_2_, bf16[8,4096]{1,0:T(8,128)(2,1)S(1)} %collective-permute-done.33.refs_3_), custom_call_target="tpu_custom_call" | custom-call | flops 1000000 | bytes 1048576 | tf_op jit(solution)/shard_map/final/pallas_call | solution.py:269
  (37 shorter events, 0.6 us)
Async XLA Ops:
  0.0 29.3 %copy-start = (bf16[1,4096,1792]{2,1,0:T(8,128)(2,1)S(1)}, bf16[1,4096,1792]{2,1,0:T(8,128)(2,1)}, u32[]{:S(2)}) copy-start(bf16[1,4096,1792]{2,1,0:T(8,128)(2,1)} %param.9) | copy-start | bytes 44040196
  0.0 29.3 %copy-start.1 = (bf16[1,4096,1792]{2,1,0:T(8,128)(2,1)S(1)}, bf16[1,4096,1792]{2,1,0:T(8,128)(2,1)}, u32[]{:S(2)}) copy-start(bf16[1,4096,1792]{2,1,0:T(8,128)(2,1)} %param.10) | copy-start | bytes 44040196
  0.0 29.3 %copy-start.2 = (bf16[1,1792,4096]{2,1,0:T(8,128)(2,1)S(1)}, bf16[1,1792,4096]{2,1,0:T(8,128)(2,1)}, u32[]{:S(2)}) copy-start(bf16[1,1792,4096]{2,1,0:T(8,128)(2,1)} %param.11) | copy-start | bytes 44040196
  1.1 5.7 %collective-permute-start = (bf16[8,4224]{1,0:T(8,128)(2,1)S(1)}, bf16[8,4224]{1,0:T(8,128)(2,1)S(1)}, u32[]{:S(2)}, u32[]{:S(2)}) collective-permute-start(bf16[8,4224]{1,0:T(8,128)(2,1)S(1)} %pack.1.refs_0_), channel_id=1, source_target_pairs={{0,2},{1,3},{2,0},{3,1},{4,6},{5,7},{6,4},{7,5},{8,10},{9,11},{10,... | collective-permute-start | bytes 202760 | tf_op jit(solution)/shard_map/ppermute | solution.py:40
  4.2 6.9 %collective-permute-start.2 = (bf16[8,4224]{1,0:T(8,128)(2,1)S(1)}, bf16[8,4224]{1,0:T(8,128)(2,1)S(1)}, u32[]{:S(2)}, u32[]{:S(2)}) collective-permute-start(bf16[8,4224]{1,0:T(8,128)(2,1)S(1)} %pack.1.refs_0_), channel_id=1, source_target_pairs={{0,6},{1,7},{2,4},{3,5},{4,2},{5,3},{6,0},{7,1},{8,14},{9,15},{10,... | collective-permute-start | bytes 202760 | tf_op jit(solution)/shard_map/ppermute | solution.py:40
  6.7 6.9 %collective-permute-start.1 = (bf16[8,4224]{1,0:T(8,128)(2,1)S(1)}, bf16[8,4224]{1,0:T(8,128)(2,1)S(1)}, u32[]{:S(2)}, u32[]{:S(2)}) collective-permute-start(bf16[8,4224]{1,0:T(8,128)(2,1)S(1)} %pack.1.refs_0_), channel_id=1, source_target_pairs={{0,4},{1,5},{2,6},{3,7},{4,0},{5,1},{6,2},{7,3},{8,12},{9,13},{10,... | collective-permute-start | bytes 202760 | tf_op jit(solution)/shard_map/ppermute | solution.py:40
  7.2 8.0 %collective-permute-start.9 = (bf16[8,4096]{1,0:T(8,128)(2,1)S(1)}, bf16[8,4096]{1,0:T(8,128)(2,1)S(1)}, u32[]{:S(2)}, u32[]{:S(2)}) collective-permute-start(bf16[8,4096]{1,0:T(8,128)(2,1)S(1)} %get-tuple-element.37.refs_0_), channel_id=1, source_target_pairs={{0,1},{1,0},{2,3},{3,2},{4,5},{5,4},{6,7},{7,6},{8,9},{9,8},{10,11... | collective-permute-start | bytes 196616 | tf_op jit(solution)/shard_map/ppermute | solution.py:40
  8.9 7.1 %collective-permute-start.11 = (bf16[8,4096]{1,0:T(8,128)(2,1)S(1)}, bf16[8,4096]{1,0:T(8,128)(2,1)S(1)}, u32[]{:S(2)}, u32[]{:S(2)}) collective-permute-start(bf16[8,4096]{1,0:T(8,128)(2,1)S(1)} %get-tuple-element.39), channel_id=1, source_target_pairs={{0,9},{1,8},{2,11},{3,10},{4,13},{5,12},{6,15},{7,14},{8,1},{9,0},... | collective-permute-start | bytes 196616 | tf_op jit(solution)/shard_map/ppermute | solution.py:40
  8.9 9.0 %collective-permute-start.3 = (bf16[8,4096]{1,0:T(8,128)(2,1)S(1)}, bf16[8,4096]{1,0:T(8,128)(2,1)S(1)}, u32[]{:S(2)}, u32[]{:S(2)}) collective-permute-start(bf16[8,4096]{1,0:T(8,128)(2,1)S(1)} %get-tuple-element.39), channel_id=1, source_target_pairs={{0,8},{1,9},{2,10},{3,11},{4,12},{5,13},{6,14},{7,15},{8,0},{9,1},... | collective-permute-start | bytes 196616 | tf_op jit(solution)/shard_map/ppermute | solution.py:40
  11.2 7.4 %collective-permute-start.13 = (bf16[8,4096]{1,0:T(8,128)(2,1)S(1)}, bf16[8,4096]{1,0:T(8,128)(2,1)S(1)}, u32[]{:S(2)}, u32[]{:S(2)}) collective-permute-start(bf16[8,4096]{1,0:T(8,128)(2,1)S(1)} %get-tuple-element.41), channel_id=1, source_target_pairs={{0,17},{1,16},{2,19},{3,18},{4,21},{5,20},{6,23},{7,22},{8,25},{9,... | collective-permute-start | bytes 196616 | tf_op jit(solution)/shard_map/ppermute | solution.py:40
  13.6 5.4 %collective-permute-start.5 = (bf16[8,4096]{1,0:T(8,128)(2,1)S(1)}, bf16[8,4096]{1,0:T(8,128)(2,1)S(1)}, u32[]{:S(2)}, u32[]{:S(2)}) collective-permute-start(bf16[8,4096]{1,0:T(8,128)(2,1)S(1)} %get-tuple-element.41), channel_id=1, source_target_pairs={{0,16},{1,17},{2,18},{3,19},{4,20},{5,21},{6,22},{7,23},{8,24},{9,... | collective-permute-start | bytes 196616 | tf_op jit(solution)/shard_map/ppermute | solution.py:40
  15.2 5.3 %collective-permute-start.15 = (bf16[8,4096]{1,0:T(8,128)(2,1)S(1)}, bf16[8,4096]{1,0:T(8,128)(2,1)S(1)}, u32[]{:S(2)}, u32[]{:S(2)}) collective-permute-start(bf16[8,4096]{1,0:T(8,128)(2,1)S(1)} %get-tuple-element.43), channel_id=1, source_target_pairs={{0,25},{1,24},{2,27},{3,26},{4,29},{5,28},{6,31},{7,30},{8,17},{9,... | collective-permute-start | bytes 196616 | tf_op jit(solution)/shard_map/ppermute | solution.py:40
  16.1 6.0 %collective-permute-start.7 = (bf16[8,4096]{1,0:T(8,128)(2,1)S(1)}, bf16[8,4096]{1,0:T(8,128)(2,1)S(1)}, u32[]{:S(2)}, u32[]{:S(2)}) collective-permute-start(bf16[8,4096]{1,0:T(8,128)(2,1)S(1)} %get-tuple-element.43), channel_id=1, source_target_pairs={{0,24},{1,25},{2,26},{3,27},{4,28},{5,29},{6,30},{7,31},{8,16},{9,... | collective-permute-start | bytes 196616 | tf_op jit(solution)/shard_map/ppermute | solution.py:40
  18.0 5.6 %collective-permute-start.10 = (bf16[8,4096]{1,0:T(8,128)(2,1)S(1)}, bf16[8,4096]{1,0:T(8,128)(2,1)S(1)}, u32[]{:S(2)}, u32[]{:S(2)}) collective-permute-start(bf16[8,4096]{1,0:T(8,128)(2,1)S(1)} %get-tuple-element.38.refs_1_), channel_id=1, source_target_pairs={{0,1},{1,0},{2,3},{3,2},{4,5},{5,4},{6,7},{7,6},{8,9},{9,8},{10,11... | collective-permute-start | bytes 196616 | tf_op jit(solution)/shard_map/ppermute | solution.py:40
  18.5 5.1 %collective-permute-start.12 = (bf16[8,4096]{1,0:T(8,128)(2,1)S(1)}, bf16[8,4096]{1,0:T(8,128)(2,1)S(1)}, u32[]{:S(2)}, u32[]{:S(2)}) collective-permute-start(bf16[8,4096]{1,0:T(8,128)(2,1)S(1)} %get-tuple-element.40), channel_id=1, source_target_pairs={{0,9},{1,8},{2,11},{3,10},{4,13},{5,12},{6,15},{7,14},{8,1},{9,0},... | collective-permute-start | bytes 196616 | tf_op jit(solution)/shard_map/ppermute | solution.py:40
  19.0 6.2 %collective-permute-start.4 = (bf16[8,4096]{1,0:T(8,128)(2,1)S(1)}, bf16[8,4096]{1,0:T(8,128)(2,1)S(1)}, u32[]{:S(2)}, u32[]{:S(2)}) collective-permute-start(bf16[8,4096]{1,0:T(8,128)(2,1)S(1)} %get-tuple-element.40), channel_id=1, source_target_pairs={{0,8},{1,9},{2,10},{3,11},{4,12},{5,13},{6,14},{7,15},{8,0},{9,1},... | collective-permute-start | bytes 196616 | tf_op jit(solution)/shard_map/ppermute | solution.py:40
  20.5 5.6 %collective-permute-start.14 = (bf16[8,4096]{1,0:T(8,128)(2,1)S(1)}, bf16[8,4096]{1,0:T(8,128)(2,1)S(1)}, u32[]{:S(2)}, u32[]{:S(2)}) collective-permute-start(bf16[8,4096]{1,0:T(8,128)(2,1)S(1)} %get-tuple-element.42), channel_id=1, source_target_pairs={{0,17},{1,16},{2,19},{3,18},{4,21},{5,20},{6,23},{7,22},{8,25},{9,... | collective-permute-start | bytes 196616 | tf_op jit(solution)/shard_map/ppermute | solution.py:40
  22.0 5.0 %collective-permute-start.6 = (bf16[8,4096]{1,0:T(8,128)(2,1)S(1)}, bf16[8,4096]{1,0:T(8,128)(2,1)S(1)}, u32[]{:S(2)}, u32[]{:S(2)}) collective-permute-start(bf16[8,4096]{1,0:T(8,128)(2,1)S(1)} %get-tuple-element.42), channel_id=1, source_target_pairs={{0,16},{1,17},{2,18},{3,19},{4,20},{5,21},{6,22},{7,23},{8,24},{9,... | collective-permute-start | bytes 196616 | tf_op jit(solution)/shard_map/ppermute | solution.py:40
  23.6 4.8 %collective-permute-start.16 = (bf16[8,4096]{1,0:T(8,128)(2,1)S(1)}, bf16[8,4096]{1,0:T(8,128)(2,1)S(1)}, u32[]{:S(2)}, u32[]{:S(2)}) collective-permute-start(bf16[8,4096]{1,0:T(8,128)(2,1)S(1)} %get-tuple-element.44), channel_id=1, source_target_pairs={{0,25},{1,24},{2,27},{3,26},{4,29},{5,28},{6,31},{7,30},{8,17},{9,... | collective-permute-start | bytes 196616 | tf_op jit(solution)/shard_map/ppermute | solution.py:40
  23.6 5.7 %collective-permute-start.8 = (bf16[8,4096]{1,0:T(8,128)(2,1)S(1)}, bf16[8,4096]{1,0:T(8,128)(2,1)S(1)}, u32[]{:S(2)}, u32[]{:S(2)}) collective-permute-start(bf16[8,4096]{1,0:T(8,128)(2,1)S(1)} %get-tuple-element.44), channel_id=1, source_target_pairs={{0,24},{1,25},{2,26},{3,27},{4,28},{5,29},{6,30},{7,31},{8,16},{9,... | collective-permute-start | bytes 196616 | tf_op jit(solution)/shard_map/ppermute | solution.py:40
  29.3 16.1 %copy-start.3 = (bf16[4096,4]{0,1:T(4,128)(2,1)S(1)}, bf16[4096,4]{0,1:T(4,128)(2,1)}, u32[]{:S(2)}) copy-start(bf16[4096,4]{0,1:T(4,128)(2,1)} %param.7) | copy-start | bytes 98308
  37.6 3.7 %collective-permute-start.17 = (bf16[8,4096]{1,0:T(8,128)(2,1)S(1)}, bf16[8,4096]{1,0:T(8,128)(2,1)S(1)}, u32[]{:S(2)}, u32[]{:S(2)}) collective-permute-start(bf16[8,4096]{1,0:T(8,128)(2,1)S(1)} %get-tuple-element.46), channel_id=1, source_target_pairs={{0,8},{1,9},{2,10},{3,11},{4,12},{5,13},{6,14},{7,15},{8,0},{9,1},... | collective-permute-start | bytes 196616 | tf_op jit(solution)/shard_map/ppermute | solution.py:40
  37.8 4.7 %collective-permute-start.18 = (bf16[8,4096]{1,0:T(8,128)(2,1)S(1)}, bf16[8,4096]{1,0:T(8,128)(2,1)S(1)}, u32[]{:S(2)}, u32[]{:S(2)}) collective-permute-start(bf16[8,4096]{1,0:T(8,128)(2,1)S(1)} %get-tuple-element.47), channel_id=1, source_target_pairs={{0,16},{1,17},{2,18},{3,19},{4,20},{5,21},{6,22},{7,23},{8,24},{9,... | collective-permute-start | bytes 196616 | tf_op jit(solution)/shard_map/ppermute | solution.py:40
  38.9 5.1 %collective-permute-start.19 = (bf16[8,4096]{1,0:T(8,128)(2,1)S(1)}, bf16[8,4096]{1,0:T(8,128)(2,1)S(1)}, u32[]{:S(2)}, u32[]{:S(2)}) collective-permute-start(bf16[8,4096]{1,0:T(8,128)(2,1)S(1)} %get-tuple-element.48), channel_id=1, source_target_pairs={{0,24},{1,25},{2,26},{3,27},{4,28},{5,29},{6,30},{7,31},{8,16},{9,... | collective-permute-start | bytes 196616 | tf_op jit(solution)/shard_map/ppermute | solution.py:40
  39.5 4.8 %collective-permute-start.20 = (bf16[8,4096]{1,0:T(8,128)(2,1)S(1)}, bf16[8,4096]{1,0:T(8,128)(2,1)S(1)}, u32[]{:S(2)}, u32[]{:S(2)}) collective-permute-start(bf16[8,4096]{1,0:T(8,128)(2,1)S(1)} %get-tuple-element.49), channel_id=1, source_target_pairs={{0,1},{1,0},{2,3},{3,2},{4,5},{5,4},{6,7},{7,6},{8,9},{9,8},{10,11... | collective-permute-start | bytes 196616 | tf_op jit(solution)/shard_map/ppermute | solution.py:40
  40.5 5.2 %collective-permute-start.21 = (bf16[8,4096]{1,0:T(8,128)(2,1)S(1)}, bf16[8,4096]{1,0:T(8,128)(2,1)S(1)}, u32[]{:S(2)}, u32[]{:S(2)}) collective-permute-start(bf16[8,4096]{1,0:T(8,128)(2,1)S(1)} %get-tuple-element.50), channel_id=1, source_target_pairs={{0,9},{1,8},{2,11},{3,10},{4,13},{5,12},{6,15},{7,14},{8,1},{9,0},... | collective-permute-start | bytes 196616 | tf_op jit(solution)/shard_map/ppermute | solution.py:40
  41.3 7.5 %collective-permute-start.22 = (bf16[8,4096]{1,0:T(8,128)(2,1)S(1)}, bf16[8,4096]{1,0:T(8,128)(2,1)S(1)}, u32[]{:S(2)}, u32[]{:S(2)}) collective-permute-start(bf16[8,4096]{1,0:T(8,128)(2,1)S(1)} %get-tuple-element.51), channel_id=1, source_target_pairs={{0,17},{1,16},{2,19},{3,18},{4,21},{5,20},{6,23},{7,22},{8,25},{9,... | collective-permute-start | bytes 196616 | tf_op jit(solution)/shard_map/ppermute | solution.py:40
  42.5 6.3 %collective-permute-start.23 = (bf16[8,4096]{1,0:T(8,128)(2,1)S(1)}, bf16[8,4096]{1,0:T(8,128)(2,1)S(1)}, u32[]{:S(2)}, u32[]{:S(2)}) collective-permute-start(bf16[8,4096]{1,0:T(8,128)(2,1)S(1)} %get-tuple-element.52), channel_id=1, source_target_pairs={{0,25},{1,24},{2,27},{3,26},{4,29},{5,28},{6,31},{7,30},{8,17},{9,... | collective-permute-start | bytes 196616 | tf_op jit(solution)/shard_map/ppermute | solution.py:40
  43.9 5.6 %collective-permute-start.25 = (bf16[8,4096]{1,0:T(8,128)(2,1)S(1)}, bf16[8,4096]{1,0:T(8,128)(2,1)S(1)}, u32[]{:S(2)}, u32[]{:S(2)}) collective-permute-start(bf16[8,4096]{1,0:T(8,128)(2,1)S(1)} %get-tuple-element.58), channel_id=1, source_target_pairs={{0,8},{1,9},{2,10},{3,11},{4,12},{5,13},{6,14},{7,15},{8,0},{9,1},... | collective-permute-start | bytes 196616 | tf_op jit(solution)/shard_map/ppermute | solution.py:40
  44.4 7.0 %collective-permute-start.26 = (bf16[8,4096]{1,0:T(8,128)(2,1)S(1)}, bf16[8,4096]{1,0:T(8,128)(2,1)S(1)}, u32[]{:S(2)}, u32[]{:S(2)}) collective-permute-start(bf16[8,4096]{1,0:T(8,128)(2,1)S(1)} %get-tuple-element.59), channel_id=1, source_target_pairs={{0,16},{1,17},{2,18},{3,19},{4,20},{5,21},{6,22},{7,23},{8,24},{9,... | collective-permute-start | bytes 196616 | tf_op jit(solution)/shard_map/ppermute | solution.py:40
  45.7 8.1 %collective-permute-start.27 = (bf16[8,4096]{1,0:T(8,128)(2,1)S(1)}, bf16[8,4096]{1,0:T(8,128)(2,1)S(1)}, u32[]{:S(2)}, u32[]{:S(2)}) collective-permute-start(bf16[8,4096]{1,0:T(8,128)(2,1)S(1)} %get-tuple-element.60), channel_id=1, source_target_pairs={{0,24},{1,25},{2,26},{3,27},{4,28},{5,29},{6,30},{7,31},{8,16},{9,... | collective-permute-start | bytes 196616 | tf_op jit(solution)/shard_map/ppermute | solution.py:40
  48.8 5.7 %collective-permute-start.28 = (bf16[8,4096]{1,0:T(8,128)(2,1)S(1)}, bf16[8,4096]{1,0:T(8,128)(2,1)S(1)}, u32[]{:S(2)}, u32[]{:S(2)}) collective-permute-start(bf16[8,4096]{1,0:T(8,128)(2,1)S(1)} %get-tuple-element.61), channel_id=1, source_target_pairs={{0,1},{1,0},{2,3},{3,2},{4,5},{5,4},{6,7},{7,6},{8,9},{9,8},{10,11... | collective-permute-start | bytes 196616 | tf_op jit(solution)/shard_map/ppermute | solution.py:40
  48.8 5.7 %collective-permute-start.29 = (bf16[8,4096]{1,0:T(8,128)(2,1)S(1)}, bf16[8,4096]{1,0:T(8,128)(2,1)S(1)}, u32[]{:S(2)}, u32[]{:S(2)}) collective-permute-start(bf16[8,4096]{1,0:T(8,128)(2,1)S(1)} %get-tuple-element.62), channel_id=1, source_target_pairs={{0,9},{1,8},{2,11},{3,10},{4,13},{5,12},{6,15},{7,14},{8,1},{9,0},... | collective-permute-start | bytes 196616 | tf_op jit(solution)/shard_map/ppermute | solution.py:40
  49.5 5.4 %collective-permute-start.30 = (bf16[8,4096]{1,0:T(8,128)(2,1)S(1)}, bf16[8,4096]{1,0:T(8,128)(2,1)S(1)}, u32[]{:S(2)}, u32[]{:S(2)}) collective-permute-start(bf16[8,4096]{1,0:T(8,128)(2,1)S(1)} %get-tuple-element.63), channel_id=1, source_target_pairs={{0,17},{1,16},{2,19},{3,18},{4,21},{5,20},{6,23},{7,22},{8,25},{9,... | collective-permute-start | bytes 196616 | tf_op jit(solution)/shard_map/ppermute | solution.py:40
  51.4 5.5 %collective-permute-start.31 = (bf16[8,4096]{1,0:T(8,128)(2,1)S(1)}, bf16[8,4096]{1,0:T(8,128)(2,1)S(1)}, u32[]{:S(2)}, u32[]{:S(2)}) collective-permute-start(bf16[8,4096]{1,0:T(8,128)(2,1)S(1)} %get-tuple-element.64), channel_id=1, source_target_pairs={{0,25},{1,24},{2,27},{3,26},{4,29},{5,28},{6,31},{7,30},{8,17},{9,... | collective-permute-start | bytes 196616 | tf_op jit(solution)/shard_map/ppermute | solution.py:40
  53.8 6.4 %collective-permute-start.24 = (bf16[8,4096]{1,0:T(8,128)(2,1)S(1)}, bf16[8,4096]{1,0:T(8,128)(2,1)S(1)}, u32[]{:S(2)}, u32[]{:S(2)}) collective-permute-start(bf16[8,4096]{1,0:T(8,128)(2,1)S(1)} %get-tuple-element.56), channel_id=1, source_target_pairs={{0,2},{1,3},{2,0},{3,1},{4,6},{5,7},{6,4},{7,5},{8,10},{9,11},{10,... | collective-permute-start | bytes 196616 | tf_op jit(solution)/shard_map/ppermute | solution.py:40
  57.1 7.5 %collective-permute-start.32 = (bf16[8,4096]{1,0:T(8,128)(2,1)S(1)}, bf16[8,4096]{1,0:T(8,128)(2,1)S(1)}, u32[]{:S(2)}, u32[]{:S(2)}) collective-permute-start(bf16[8,4096]{1,0:T(8,128)(2,1)S(1)} %get-tuple-element.67), channel_id=1, source_target_pairs={{0,4},{1,5},{2,6},{3,7},{4,0},{5,1},{6,2},{7,3},{8,12},{9,13},{10,... | collective-permute-start | bytes 196616 | tf_op jit(solution)/shard_map/ppermute | solution.py:40
  59.4 6.1 %collective-permute-start.33 = (bf16[8,4096]{1,0:T(8,128)(2,1)S(1)}, bf16[8,4096]{1,0:T(8,128)(2,1)S(1)}, u32[]{:S(2)}, u32[]{:S(2)}) collective-permute-start(bf16[8,4096]{1,0:T(8,128)(2,1)S(1)} %get-tuple-element.68), channel_id=1, source_target_pairs={{0,6},{1,7},{2,4},{3,5},{4,2},{5,3},{6,0},{7,1},{8,14},{9,15},{10,... | collective-permute-start | bytes 196616 | tf_op jit(solution)/shard_map/ppermute | solution.py:40

commit v2 on v1

--- a/solution.py
+++ b/solution.py
@@ -85,16 +85,17 @@
     )
 
 
-def dispatch_kernel(blocks, n_experts, width, *refs):
+def dispatch_kernel(blocks, n_experts, width, wanted, *refs):
     packed = gather_blocks(refs[:blocks])
     out_refs = refs[blocks:]
     slots_per = packed.shape[0] // blocks // 2
     per_expert = blocks * slots_per
     lanes = ids_to_lanes(packed[:, width:], blocks)
     chosen, _ = picks(lanes, lax.axis_index("expert"), n_experts, blocks, slots_per)
-    rows = dot(chosen.astype(jnp.bfloat16), packed[:, :width]).astype(jnp.bfloat16)
-    for k in range(n_experts):
-        out_refs[k][...] = rows[k * per_expert : (k + 1) * per_expert]
+    rows = dot(chosen.astype(jnp.bfloat16), packed[:, :width])
+    for out_ref, (k, first, count) in zip(out_refs, wanted):
+        start = k * per_expert + first
+        out_ref[...] = rows[start : start + count].astype(jnp.bfloat16)
 
 
 def pack_kernel(tokens_ref, ids_ref, packed_ref):
@@ -125,17 +126,18 @@
     low_ref[...] = (weights - high.astype(jnp.float32)).astype(jnp.bfloat16)
 
 
-def ffn_kernel(parts, halves, tile_width, out_tile, *refs):
-    pieces = parts * halves
+def ffn_kernel(piece_counts, tile_width, out_tile, *refs):
+    pieces = sum(piece_counts)
     row_refs = refs[:pieces]
     gate_ref, up_ref, down_ref = refs[pieces : pieces + 3]
     out_refs = refs[pieces + 3 : 2 * pieces + 3]
     rows, hidden = refs[2 * pieces + 3 :]
-    per_piece = row_refs[0].shape[0]
-    per_part = per_piece * halves
-    for part in range(parts):
-        mine = row_refs[part * halves : (part + 1) * halves]
+    per_part = rows.shape[0] // len(piece_counts)
+    taken = 0
+    for part, count in enumerate(piece_counts):
+        mine = row_refs[taken : taken + count]
         rows[pl.ds(part * per_part, per_part), :] = gather_blocks(mine)
+        taken += count
 
     @pl.loop(0, hidden.shape[1] // tile_width)
     def _(tile):
@@ -148,16 +150,23 @@
     def _(tile):
         columns = pl.ds(pl.multiple_of(tile * out_tile, out_tile), out_tile)
         result = dot(hidden[...], down_ref[:, columns])
-        for piece in range(pieces):
-            mine = result[piece * per_piece : (piece + 1) * per_piece]
-            out_refs[piece][:, columns] = mine.astype(jnp.bfloat16)
-
-
-def combine_kernel(parts, n_experts, blocks, *refs):
+        first = 0
+        for out_ref in out_refs:
+            count = out_ref.shape[0]
+            out_ref[:, columns] = result[first : first + count].astype(jnp.bfloat16)
+            first += count
+
+
+def combine_kernel(parts, n_experts, blocks, half, *refs):
     high_ref, low_ref = refs[parts : parts + 2]
     out_refs = refs[parts + 2 :]
     inner = parts // n_experts
-    rows = gather_blocks(refs[:parts])
+    count = high_ref.shape[0] // n_experts
+    rows = []
+    for ref in refs[:parts]:
+        first = half * count if ref.shape[0] > count else 0
+        rows.append(ref[...].astype(jnp.float32)[first : first + count])
+    rows = jnp.concatenate(rows, axis=0).astype(jnp.bfloat16)
     high = jnp.concatenate([high_ref[...]] * inner, axis=0)
     low = jnp.concatenate([low_ref[...]] * inner, axis=0)
     mixed = dot(high, rows, (0, 0)) + dot(low, rows, (0, 0))
@@ -209,15 +218,18 @@
     piece_rows = per_half * slots_per
     order = [(i, k) for i in range(inner) for k in range(n_experts)]
 
-    def dispatch(half):
-        return pl.pallas_call(
-            functools.partial(dispatch_kernel, per_half, n_experts, width),
-            out_shape=[jax.ShapeDtypeStruct((piece_rows, width), bf16)] * n_experts,
-            in_specs=[vmem] * per_half,
-            out_specs=[vmem] * n_experts,
-            compiler_params=pltpu.CompilerParams(vmem_limit_bytes=6 * MIB),
+    split, whole = plane_groups(inner, n_experts)
+
+    def dispatch(blocks, wanted):
+        outs = pl.pallas_call(
+            functools.partial(dispatch_kernel, blocks, n_experts, width, tuple(wanted)),
+            out_shape=[jax.ShapeDtypeStruct((w[2], width), bf16) for w in wanted],
+            in_specs=[vmem] * blocks,
+            out_specs=[vmem] * len(wanted),
+            compiler_params=pltpu.CompilerParams(vmem_limit_bytes=8 * MIB),
             cost_estimate=cost(4e8, 4 * MIB),
-        )(*along[half * per_half : (half + 1) * per_half])
+        )(*along[:blocks])
+        return dict(zip(wanted, outs))
 
     def weights(half):
         n_tokens = per_half * local_tokens
@@ -230,41 +242,59 @@
             cost_estimate=cost(4e8, MIB),
         )(*along[half * per_half : (half + 1) * per_half], router.T)
 
-    arrived = []
-    for half in range(halves):
-        buffers = dispatch(half)
-        arrived.append(
-            [buffers[k] if (i, k) == (0, 0) else exchange(buffers[k], k, i) for i, k in order]
-        )
+    split_experts = sorted({k for _, k in split})
+    whole_experts = sorted({k for _, k in whole} | {0})
+    near_rows = dispatch(per_half, [(k, 0, piece_rows) for k in split_experts])
+    late_rows = dispatch(
+        outer,
+        [(k, piece_rows, piece_rows) for k in split_experts]
+        + [(k, 0, per_expert) for k in whole_experts],
+    )
+    row_pieces = []
+    for i, k in order:
+        if (i, k) in split:
+            row_pieces.append(exchange(near_rows[k, 0, piece_rows], k, i))
+            row_pieces.append(exchange(late_rows[k, piece_rows, piece_rows], k, i))
+        elif (i, k) == (0, 0):
+            row_pieces.append(late_rows[k, 0, per_expert])
+        else:
+            row_pieces.append(exchange(late_rows[k, 0, per_expert], k, i))
+    piece_counts = tuple(2 if p in split else 1 for p in order)
     combine_weights = [weights(half) for half in range(halves)]
 
-    pieces = parts * halves
     sent = pl.pallas_call(
-        functools.partial(ffn_kernel, parts, halves, tile_width, OUT_TILE),
+        functools.partial(ffn_kernel, piece_counts, tile_width, OUT_TILE),
         name="ffn",
-        out_shape=[jax.ShapeDtypeStruct((piece_rows, width), bf16)] * pieces,
-        in_specs=[vmem] * (pieces + 3),
-        out_specs=[vmem] * pieces,
+        out_shape=[jax.ShapeDtypeStruct(piece.shape, bf16) for piece in row_pieces],
+        in_specs=[vmem] * (len(row_pieces) + 3),
+        out_specs=[vmem] * len(row_pieces),
         scratch_shapes=[pltpu.VMEM((n_rows, width), bf16), pltpu.VMEM((n_rows, n_hidden), bf16)],
         compiler_params=pltpu.CompilerParams(vmem_limit_bytes=5 * MIB),
         cost_estimate=cost(6 * n_rows * width * n_hidden, 6 * width * n_hidden),
-    )(*(arrived[half][j] for j in range(parts) for half in range(halves)), w_gate, w_up, w_down)
-
+    )(*row_pieces, w_gate, w_up, w_down)
+
+    back = ([], [])
+    left = list(sent)
+    for i, k in order:
+        if (i, k) in split:
+            back[0].append(exchange(left.pop(0), k, i))
+            back[1].append(exchange(left.pop(0), k, i))
+        else:
+            mine = left.pop(0)
+            if (i, k) != (0, 0):
+                mine = exchange(mine, k, i)
+            back[0].append(mine)
+            back[1].append(mine)
     mixed = []
     for half in range(halves):
-        mine = sent[half::halves]
-        back = [
-            mine[j] if (i, k) == (0, 0) else exchange(mine[j], k, i)
-            for j, (i, k) in enumerate(order)
-        ]
         mixed += pl.pallas_call(
-            functools.partial(combine_kernel, parts, n_experts, per_half),
+            functools.partial(combine_kernel, parts, n_experts, per_half, half),
             out_shape=[jax.ShapeDtypeStruct((local_tokens, width), bf16)] * per_half,
             in_specs=[vmem] * (parts + 2),
             out_specs=[vmem] * per_half,
             compiler_params=pltpu.CompilerParams(vmem_limit_bytes=20 * MIB),
             cost_estimate=cost(4e8, 4 * MIB),
-        )(*back, *combine_weights[half])
+        )(*back[half], *combine_weights[half])
     home = [mixed[0]] + [exchange(mixed[d], 0, d * inner) for d in range(1, outer)]
     return pl.pallas_call(
         final_kernel,
@@ -277,6 +307,18 @@
     )(*home)
 
 
+def plane_groups(inner, n_experts):
+    others = [(i, k) for i in range(inner) for k in range(n_experts) if (i, k) != (0, 0)]
+    far = [p for p in others if p[0] and p[1] > 1]
+    near = [p for p in others if not p[0] and p[1] < 2]
+    by_k = [p for p in others if not p[0] and p[1] > 1]
+    by_i = [p for p in others if p[0] and p[1] < 2]
+    pairs = [p for pair in zip(by_k, by_i) for p in pair]
+    pairs += by_k[len(by_i) :] + by_i[len(by_k) :]
+    count = len(pairs) // 2
+    return far + pairs[:count], pairs[count:] + near
+
+
 def solution(mesh):
     placed = (
         P(("expert", "shard"), None),

time: 66.2 us -> 59.7 us (0.902)
  starting transfers between devices: 40 us -> 33 us
    ppermute x34 -> x28, starting transfers between devices: 40 us -> 33 us  [swap(): return lax.ppermute(value, ('expert', 'shard'), pairs)]
    ppermute x34 -> x28, waiting for transfers between devices: 13.8 us -> 14.4 us  [swap(): return lax.ppermute(value, ('expert', 'shard'), pairs)]
  transfers between devices with their start and end apart: 34 -> 28, of which waited for: 11 -> 11; matrix products, arithmetic and copies ran while one was open for 0% -> 0% of each run, Pallas kernels for 3% -> 4%
where the time goes in v2:
time: 59.7 us; the launch traced here: 59.6 us
  starting transfers between devices  33 us (55%)
  waiting for transfers between devices  14.4 us (24%)
  Pallas kernels  12 us (20%)
    ppermute x28, starting transfers between devices, swap(): return lax.ppermute(value, ('expert', 'shard'), pairs)  33 us
    ppermute x28, waiting for transfers between devices, swap(): return lax.ppermute(value, ('expert', 'shard'), pairs)  14.4 us
    pallas_call x1, Pallas kernels, shards_program(): pl.pallas_call(functools.partial(ffn_kernel, piece_counts, tile_width, OU...  8.07 us
  transfers between devices with their start and end apart: 28, of which 11 were waited for; matrix products, arithmetic and copies ran while one was open for 0% of the time, Pallas kernels for 4%

profile of v2, /device:TPU:0, one launch (start us, length us, event | category | flops | bytes accessed | tf_op | source)
XLA Modules:
  0.0 59.6 jit_solution(8316258139282481818)
XLA Ops:
  0.0 1.1 %pack.1.refs_0_ = bf16[8,4224]{1,0:T(8,128)(2,1)S(1)} custom-call(bf16[8,4096]{1,0:T(8,128)(2,1)} %tokens_ref.1, s32[2,8]{1,0:T(2,128)} %bitcast.10), custom_call_target="tpu_custom_call" | custom-call | flops 60000002048 | bytes 1048576 | tf_op jit(solution)/shard_map/pack/pallas_call | solution.py:204
  1.1 3.1 %collective-permute-start = (bf16[8,4224]{1,0:T(8,128)(2,1)S(1)}, bf16[8,4224]{1,0:T(8,128)(2,1)S(1)}, u32[]{:S(2)}, u32[]{:S(2)}) collective-permute-start(bf16[8,4224]{1,0:T(8,128)(2,1)S(1)} %pack.1.refs_0_), channel_id=1, source_target_pairs={{0,2},{1,3},{2,0},{3,1},{4,6},{5,7},{6,4},{7,5},{8,10},{9,11},{10,... | collective-permute-start | bytes 202760 | tf_op jit(solution)/shard_map/ppermute | solution.py:40
  4.2 2.5 %collective-permute-start.2 = (bf16[8,4224]{1,0:T(8,128)(2,1)S(1)}, bf16[8,4224]{1,0:T(8,128)(2,1)S(1)}, u32[]{:S(2)}, u32[]{:S(2)}) collective-permute-start(bf16[8,4224]{1,0:T(8,128)(2,1)S(1)} %pack.1.refs_0_), channel_id=1, source_target_pairs={{0,6},{1,7},{2,4},{3,5},{4,2},{5,3},{6,0},{7,1},{8,14},{9,15},{10,... | collective-permute-start | bytes 202760 | tf_op jit(solution)/shard_map/ppermute | solution.py:40
  6.7 0.1 collective-permute-start.1
  6.8 0.0 collective-permute-done.refs_1_
  6.8 0.4 shard_map.65
  7.2 1.7 %collective-permute-start.7 = (bf16[8,4096]{1,0:T(8,128)(2,1)S(1)}, bf16[8,4096]{1,0:T(8,128)(2,1)S(1)}, u32[]{:S(2)}, u32[]{:S(2)}) collective-permute-start(bf16[8,4096]{1,0:T(8,128)(2,1)S(1)} %get-tuple-element.39), channel_id=1, source_target_pairs={{0,1},{1,0},{2,3},{3,2},{4,5},{5,4},{6,7},{7,6},{8,9},{9,8},{10,11... | collective-permute-start | bytes 196616 | tf_op jit(solution)/shard_map/ppermute | solution.py:40
  8.9 1.4 %collective-permute-start.10 = (bf16[8,4096]{1,0:T(8,128)(2,1)S(1)}, bf16[8,4096]{1,0:T(8,128)(2,1)S(1)}, u32[]{:S(2)}, u32[]{:S(2)}) collective-permute-start(bf16[8,4096]{1,0:T(8,128)(2,1)S(1)} %get-tuple-element.36), channel_id=1, source_target_pairs={{0,17},{1,16},{2,19},{3,18},{4,21},{5,20},{6,23},{7,22},{8,25},{9,... | collective-permute-start | bytes 196616 | tf_op jit(solution)/shard_map/ppermute | solution.py:40
  10.4 0.8 %collective-permute-done.2.refs_3_.refs_1_ = bf16[8,4224]{1,0:T(8,128)(2,1)S(1)} collective-permute-done((bf16[8,4224]{1,0:T(8,128)(2,1)S(1)}, bf16[8,4224]{1,0:T(8,128)(2,1)S(1)}, u32[]{:S(2)}, u32[]{:S(2)}) %collective-permute-start.2) | collective-permute-done | bytes 67616 | tf_op jit(solution)/shard_map/ppermute | solution.py:40
  11.2 1.5 %collective-permute-start.4 = (bf16[8,4096]{1,0:T(8,128)(2,1)S(1)}, bf16[8,4096]{1,0:T(8,128)(2,1)S(1)}, u32[]{:S(2)}, u32[]{:S(2)}) collective-permute-start(bf16[8,4096]{1,0:T(8,128)(2,1)S(1)} %get-tuple-element.36), channel_id=1, source_target_pairs={{0,16},{1,17},{2,18},{3,19},{4,20},{5,21},{6,22},{7,23},{8,24},{9,... | collective-permute-start | bytes 196616 | tf_op jit(solution)/shard_map/ppermute | solution.py:40
  12.6 0.6 %collective-permute-done.1.refs_2_.refs_0_ = bf16[8,4224]{1,0:T(8,128)(2,1)S(1)} collective-permute-done((bf16[8,4224]{1,0:T(8,128)(2,1)S(1)}, bf16[8,4224]{1,0:T(8,128)(2,1)S(1)}, u32[]{:S(2)}, u32[]{:S(2)}) %collective-permute-start.1) | collective-permute-done | bytes 67616 | tf_op jit(solution)/shard_map/ppermute | solution.py:40
  13.3 0.5 shard_map.64
  13.8 1.6 %collective-permute-start.8 = (bf16[8,4096]{1,0:T(8,128)(2,1)S(1)}, bf16[8,4096]{1,0:T(8,128)(2,1)S(1)}, u32[]{:S(2)}, u32[]{:S(2)}) collective-permute-start(bf16[8,4096]{1,0:T(8,128)(2,1)S(1)} %get-tuple-element.40), channel_id=1, source_target_pairs={{0,1},{1,0},{2,3},{3,2},{4,5},{5,4},{6,7},{7,6},{8,9},{9,8},{10,11... | collective-permute-start | bytes 196616 | tf_op jit(solution)/shard_map/ppermute | solution.py:40
  15.4 0.7 %collective-permute-start.13 = (bf16[8,4096]{1,0:T(8,128)(2,1)S(1)}, bf16[8,4096]{1,0:T(8,128)(2,1)S(1)}, u32[]{:S(2)}, u32[]{:S(2)}) collective-permute-start(bf16[8,4096]{1,0:T(8,128)(2,1)S(1)} %get-tuple-element.42), channel_id=1, source_target_pairs={{0,25},{1,24},{2,27},{3,26},{4,29},{5,28},{6,31},{7,30},{8,17},{9,... | collective-permute-start | bytes 196616 | tf_op jit(solution)/shard_map/ppermute | solution.py:40
  16.1 1.0 %collective-permute-start.6 = (bf16[16,4096]{1,0:T(8,128)(2,1)S(1)}, bf16[16,4096]{1,0:T(8,128)(2,1)S(1)}, u32[]{:S(2)}, u32[]{:S(2)}) collective-permute-start(bf16[16,4096]{1,0:T(8,128)(2,1)S(1)} %get-tuple-element.38), channel_id=1, source_target_pairs={{0,24},{1,25},{2,26},{3,27},{4,28},{5,29},{6,30},{7,31},{8,16},{9,... | collective-permute-start | bytes 393224 | tf_op jit(solution)/shard_map/ppermute | solution.py:40
  17.1 1.0 %collective-permute-start.9 = (bf16[16,4096]{1,0:T(8,128)(2,1)S(1)}, bf16[16,4096]{1,0:T(8,128)(2,1)S(1)}, u32[]{:S(2)}, u32[]{:S(2)}) collective-permute-start(bf16[16,4096]{1,0:T(8,128)(2,1)S(1)} %get-tuple-element.35), channel_id=1, source_target_pairs={{0,9},{1,8},{2,11},{3,10},{4,13},{5,12},{6,15},{7,14},{8,1},{9,0},... | collective-permute-start | bytes 393224 | tf_op jit(solution)/shard_map/ppermute | solution.py:40
  18.1 0.6 collective-permute-start.3
  18.7 1.9 %collective-permute-start.11 = (bf16[8,4096]{1,0:T(8,128)(2,1)S(1)}, bf16[8,4096]{1,0:T(8,128)(2,1)S(1)}, u32[]{:S(2)}, u32[]{:S(2)}) collective-permute-start(bf16[8,4096]{1,0:T(8,128)(2,1)S(1)} %get-tuple-element.37), channel_id=1, source_target_pairs={{0,17},{1,16},{2,19},{3,18},{4,21},{5,20},{6,23},{7,22},{8,25},{9,... | collective-permute-start | bytes 196616 | tf_op jit(solution)/shard_map/ppermute | solution.py:40
  20.6 1.6 %collective-permute-start.5 = (bf16[8,4096]{1,0:T(8,128)(2,1)S(1)}, bf16[8,4096]{1,0:T(8,128)(2,1)S(1)}, u32[]{:S(2)}, u32[]{:S(2)}) collective-permute-start(bf16[8,4096]{1,0:T(8,128)(2,1)S(1)} %get-tuple-element.37), channel_id=1, source_target_pairs={{0,16},{1,17},{2,18},{3,19},{4,20},{5,21},{6,22},{7,23},{8,24},{9,... | collective-permute-start | bytes 196616 | tf_op jit(solution)/shard_map/ppermute | solution.py:40
  22.2 3.1 %collective-permute-done.11.refs_9_ = bf16[8,4096]{1,0:T(8,128)(2,1)S(1)} collective-permute-done((bf16[8,4096]{1,0:T(8,128)(2,1)S(1)}, bf16[8,4096]{1,0:T(8,128)(2,1)S(1)}, u32[]{:S(2)}, u32[]{:S(2)}) %collective-permute-start.11) | collective-permute-done | bytes 65568 | tf_op jit(solution)/shard_map/ppermute | solution.py:40
  25.3 0.1 collective-permute-done.5.refs_3_
  25.4 0.0 copy-start.3
  25.4 8.1 %ffn.1 = (bf16[16,4096]{1,0:T(8,128)(2,1)S(1)}, bf16[16,4096]{1,0:T(8,128)(2,1)S(1)}, bf16[8,4096]{1,0:T(8,128)(2,1)S(1)}, bf16[8,4096]{1,0:T(8,128)(2,1)S(1)}, ...) custom-call(bf16[16,4096]{1,0:T(8,128)(2,1)S(1)} %get-tuple-element., ...), custom_call_target="tpu_custom_call" | custom-call | flops 5637144576 | bytes 44040192 | tf_op jit(solution)/shard_map/ffn/pallas_call | solution.py:265
  33.5 1.4 %collective-permute-start.22 = (bf16[8,4096]{1,0:T(8,128)(2,1)S(1)}, bf16[8,4096]{1,0:T(8,128)(2,1)S(1)}, u32[]{:S(2)}, u32[]{:S(2)}) collective-permute-start(bf16[8,4096]{1,0:T(8,128)(2,1)S(1)} %get-tuple-element.55), channel_id=1, source_target_pairs={{0,16},{1,17},{2,18},{3,19},{4,20},{5,21},{6,22},{7,23},{8,24},{9,... | collective-permute-start | bytes 196616 | tf_op jit(solution)/shard_map/ppermute | solution.py:40
  34.9 1.4 %collective-permute-start.23 = (bf16[8,4096]{1,0:T(8,128)(2,1)S(1)}, bf16[8,4096]{1,0:T(8,128)(2,1)S(1)}, u32[]{:S(2)}, u32[]{:S(2)}) collective-permute-start(bf16[8,4096]{1,0:T(8,128)(2,1)S(1)} %get-tuple-element.56), channel_id=1, source_target_pairs={{0,1},{1,0},{2,3},{3,2},{4,5},{5,4},{6,7},{7,6},{8,9},{9,8},{10,11... | collective-permute-start | bytes 196616 | tf_op jit(solution)/shard_map/ppermute | solution.py:40
  36.2 0.8 %collective-permute-start.16 = (bf16[16,4096]{1,0:T(8,128)(2,1)S(1)}, bf16[16,4096]{1,0:T(8,128)(2,1)S(1)}, u32[]{:S(2)}, u32[]{:S(2)}) collective-permute-start(bf16[16,4096]{1,0:T(8,128)(2,1)S(1)} %get-tuple-element.46), channel_id=1, source_target_pairs={{0,24},{1,25},{2,26},{3,27},{4,28},{5,29},{6,30},{7,31},{8,16},{9,... | collective-permute-start | bytes 393224 | tf_op jit(solution)/shard_map/ppermute | solution.py:40
  37.0 0.3 collective-permute-start.18
  37.3 0.5 collective-permute-done.22.refs_2_
  37.8 2.1 %collective-permute-start.24 = (bf16[8,4096]{1,0:T(8,128)(2,1)S(1)}, bf16[8,4096]{1,0:T(8,128)(2,1)S(1)}, u32[]{:S(2)}, u32[]{:S(2)}) collective-permute-start(bf16[8,4096]{1,0:T(8,128)(2,1)S(1)} %get-tuple-element.57), channel_id=1, source_target_pairs={{0,17},{1,16},{2,19},{3,18},{4,21},{5,20},{6,23},{7,22},{8,25},{9,... | collective-permute-start | bytes 196616 | tf_op jit(solution)/shard_map/ppermute | solution.py:40
  40.0 0.1 collective-permute-start.25
  40.1 0.3 shard_map.68
  40.4 3.3 %collective-permute-done.24.refs_6_ = bf16[8,4096]{1,0:T(8,128)(2,1)S(1)} collective-permute-done((bf16[8,4096]{1,0:T(8,128)(2,1)S(1)}, bf16[8,4096]{1,0:T(8,128)(2,1)S(1)}, u32[]{:S(2)}, u32[]{:S(2)}) %collective-permute-start.24) | collective-permute-done | bytes 65568 | tf_op jit(solution)/shard_map/ppermute | solution.py:40
  43.7 0.7 %collective-permute-start.15 = (bf16[8,4096]{1,0:T(8,128)(2,1)S(1)}, bf16[8,4096]{1,0:T(8,128)(2,1)S(1)}, u32[]{:S(2)}, u32[]{:S(2)}) collective-permute-start(bf16[8,4096]{1,0:T(8,128)(2,1)S(1)} %get-tuple-element.45), channel_id=1, source_target_pairs={{0,16},{1,17},{2,18},{3,19},{4,20},{5,21},{6,22},{7,23},{8,24},{9,... | collective-permute-start | bytes 196616 | tf_op jit(solution)/shard_map/ppermute | solution.py:40
  44.3 0.8 %collective-permute-done.25.refs_7_ = bf16[8,4096]{1,0:T(8,128)(2,1)S(1)} collective-permute-done((bf16[8,4096]{1,0:T(8,128)(2,1)S(1)}, bf16[8,4096]{1,0:T(8,128)(2,1)S(1)}, u32[]{:S(2)}, u32[]{:S(2)}) %collective-permute-start.25) | collective-permute-done | bytes 65568 | tf_op jit(solution)/shard_map/ppermute | solution.py:40
  45.2 1.0 %collective-permute-start.17 = (bf16[8,4096]{1,0:T(8,128)(2,1)S(1)}, bf16[8,4096]{1,0:T(8,128)(2,1)S(1)}, u32[]{:S(2)}, u32[]{:S(2)}) collective-permute-start(bf16[8,4096]{1,0:T(8,128)(2,1)S(1)} %get-tuple-element.47), channel_id=1, source_target_pairs={{0,1},{1,0},{2,3},{3,2},{4,5},{5,4},{6,7},{7,6},{8,9},{9,8},{10,11... | collective-permute-start | bytes 196616 | tf_op jit(solution)/shard_map/ppermute | solution.py:40
  46.2 1.1 %collective-permute-start.19 = (bf16[8,4096]{1,0:T(8,128)(2,1)S(1)}, bf16[8,4096]{1,0:T(8,128)(2,1)S(1)}, u32[]{:S(2)}, u32[]{:S(2)}) collective-permute-start(bf16[8,4096]{1,0:T(8,128)(2,1)S(1)} %get-tuple-element.49), channel_id=1, source_target_pairs={{0,17},{1,16},{2,19},{3,18},{4,21},{5,20},{6,23},{7,22},{8,25},{9,... | collective-permute-start | bytes 196616 | tf_op jit(solution)/shard_map/ppermute | solution.py:40
  47.3 0.8 %collective-permute-start.20 = (bf16[8,4096]{1,0:T(8,128)(2,1)S(1)}, bf16[8,4096]{1,0:T(8,128)(2,1)S(1)}, u32[]{:S(2)}, u32[]{:S(2)}) collective-permute-start(bf16[8,4096]{1,0:T(8,128)(2,1)S(1)} %get-tuple-element.50), channel_id=1, source_target_pairs={{0,25},{1,24},{2,27},{3,26},{4,29},{5,28},{6,31},{7,30},{8,17},{9,... | collective-permute-start | bytes 196616 | tf_op jit(solution)/shard_map/ppermute | solution.py:40
  48.1 0.3 shard_map.66
  48.4 0.3 shard_map.69
  48.7 2.8 %collective-permute-start.26 = (bf16[8,4096]{1,0:T(8,128)(2,1)S(1)}, bf16[8,4096]{1,0:T(8,128)(2,1)S(1)}, u32[]{:S(2)}, u32[]{:S(2)}) collective-permute-start(bf16[8,4096]{1,0:T(8,128)(2,1)S(1)} %get-tuple-element.61), channel_id=1, source_target_pairs={{0,4},{1,5},{2,6},{3,7},{4,0},{5,1},{6,2},{7,3},{8,12},{9,13},{10,... | collective-permute-start | bytes 196616 | tf_op jit(solution)/shard_map/ppermute | solution.py:40
  51.5 0.8 %collective-permute-start.27 = (bf16[8,4096]{1,0:T(8,128)(2,1)S(1)}, bf16[8,4096]{1,0:T(8,128)(2,1)S(1)}, u32[]{:S(2)}, u32[]{:S(2)}) collective-permute-start(bf16[8,4096]{1,0:T(8,128)(2,1)S(1)} %get-tuple-element.62), channel_id=1, source_target_pairs={{0,6},{1,7},{2,4},{3,5},{4,2},{5,3},{6,0},{7,1},{8,14},{9,15},{10,... | collective-permute-start | bytes 196616 | tf_op jit(solution)/shard_map/ppermute | solution.py:40
  52.3 0.3 collective-permute-done.20.refs_7_
  52.6 0.3 shard_map.67
  52.9 1.1 %collective-permute-start.21 = (bf16[8,4096]{1,0:T(8,128)(2,1)S(1)}, bf16[8,4096]{1,0:T(8,128)(2,1)S(1)}, u32[]{:S(2)}, u32[]{:S(2)}) collective-permute-start(bf16[8,4096]{1,0:T(8,128)(2,1)S(1)} %get-tuple-element.54), channel_id=1, source_target_pairs={{0,2},{1,3},{2,0},{3,1},{4,6},{5,7},{6,4},{7,5},{8,10},{9,11},{10,... | collective-permute-start | bytes 196616 | tf_op jit(solution)/shard_map/ppermute | solution.py:40
  54.0 2.0 %collective-permute-done.26.refs_2_ = bf16[8,4096]{1,0:T(8,128)(2,1)S(1)} collective-permute-done((bf16[8,4096]{1,0:T(8,128)(2,1)S(1)}, bf16[8,4096]{1,0:T(8,128)(2,1)S(1)}, u32[]{:S(2)}, u32[]{:S(2)}) %collective-permute-start.26) | collective-permute-done | bytes 65568 | tf_op jit(solution)/shard_map/ppermute | solution.py:40
  56.0 2.2 %collective-permute-done.27.refs_3_ = bf16[8,4096]{1,0:T(8,128)(2,1)S(1)} collective-permute-done((bf16[8,4096]{1,0:T(8,128)(2,1)S(1)}, bf16[8,4096]{1,0:T(8,128)(2,1)S(1)}, u32[]{:S(2)}, u32[]{:S(2)}) %collective-permute-start.27) | collective-permute-done | bytes 65568 | tf_op jit(solution)/shard_map/ppermute | solution.py:40
  58.2 0.7 %collective-permute-done.21.refs_1_ = bf16[8,4096]{1,0:T(8,128)(2,1)S(1)} collective-permute-done((bf16[8,4096]{1,0:T(8,128)(2,1)S(1)}, bf16[8,4096]{1,0:T(8,128)(2,1)S(1)}, u32[]{:S(2)}, u32[]{:S(2)}) %collective-permute-start.21) | collective-permute-done | bytes 65568 | tf_op jit(solution)/shard_map/ppermute | solution.py:40
  58.9 0.7 %final.1 = bf16[8,4096]{1,0:T(8,128)(2,1)} custom-call(bf16[8,4096]{1,0:T(8,128)(2,1)S(1)} %get-tuple-element.53.refs_0_, bf16[8,4096]{1,0:T(8,128)(2,1)S(1)} %collective-permute-done.21.refs_1_, bf16[8,4096]{1,0:T(8,128)(2,1)S(1)} %collective-permute-done.26.refs_2_, bf16[8,4096]{1,0:T(8,128)(2,1)S(1)} %collective-permute-done.27.refs_3_), custom_call_target="tpu_custom_call" | custom-call | flops 1000000 | bytes 1048576 | tf_op jit(solution)/shard_map/final/pallas_call | solution.py:299
  (25 shorter events, 0.1 us)
Async XLA Ops:
  0.0 25.4 %copy-start = (bf16[1,4096,1792]{2,1,0:T(8,128)(2,1)S(1)}, bf16[1,4096,1792]{2,1,0:T(8,128)(2,1)}, u32[]{:S(2)}) copy-start(bf16[1,4096,1792]{2,1,0:T(8,128)(2,1)} %param.9) | copy-start | bytes 44040196
  0.0 25.4 %copy-start.1 = (bf16[1,4096,1792]{2,1,0:T(8,128)(2,1)S(1)}, bf16[1,4096,1792]{2,1,0:T(8,128)(2,1)}, u32[]{:S(2)}) copy-start(bf16[1,4096,1792]{2,1,0:T(8,128)(2,1)} %param.10) | copy-start | bytes 44040196
  0.0 25.4 %copy-start.2 = (bf16[1,1792,4096]{2,1,0:T(8,128)(2,1)S(1)}, bf16[1,1792,4096]{2,1,0:T(8,128)(2,1)}, u32[]{:S(2)}) copy-start(bf16[1,1792,4096]{2,1,0:T(8,128)(2,1)} %param.11) | copy-start | bytes 44040196
  1.1 5.7 %collective-permute-start = (bf16[8,4224]{1,0:T(8,128)(2,1)S(1)}, bf16[8,4224]{1,0:T(8,128)(2,1)S(1)}, u32[]{:S(2)}, u32[]{:S(2)}) collective-permute-start(bf16[8,4224]{1,0:T(8,128)(2,1)S(1)} %pack.1.refs_0_), channel_id=1, source_target_pairs={{0,2},{1,3},{2,0},{3,1},{4,6},{5,7},{6,4},{7,5},{8,10},{9,11},{10,... | collective-permute-start | bytes 202760 | tf_op jit(solution)/shard_map/ppermute | solution.py:40
  4.2 6.9 %collective-permute-start.2 = (bf16[8,4224]{1,0:T(8,128)(2,1)S(1)}, bf16[8,4224]{1,0:T(8,128)(2,1)S(1)}, u32[]{:S(2)}, u32[]{:S(2)}) collective-permute-start(bf16[8,4224]{1,0:T(8,128)(2,1)S(1)} %pack.1.refs_0_), channel_id=1, source_target_pairs={{0,6},{1,7},{2,4},{3,5},{4,2},{5,3},{6,0},{7,1},{8,14},{9,15},{10,... | collective-permute-start | bytes 202760 | tf_op jit(solution)/shard_map/ppermute | solution.py:40
  6.7 6.6 %collective-permute-start.1 = (bf16[8,4224]{1,0:T(8,128)(2,1)S(1)}, bf16[8,4224]{1,0:T(8,128)(2,1)S(1)}, u32[]{:S(2)}, u32[]{:S(2)}) collective-permute-start(bf16[8,4224]{1,0:T(8,128)(2,1)S(1)} %pack.1.refs_0_), channel_id=1, source_target_pairs={{0,4},{1,5},{2,6},{3,7},{4,0},{5,1},{6,2},{7,3},{8,12},{9,13},{10,... | collective-permute-start | bytes 202760 | tf_op jit(solution)/shard_map/ppermute | solution.py:40
  7.2 8.1 %collective-permute-start.7 = (bf16[8,4096]{1,0:T(8,128)(2,1)S(1)}, bf16[8,4096]{1,0:T(8,128)(2,1)S(1)}, u32[]{:S(2)}, u32[]{:S(2)}) collective-permute-start(bf16[8,4096]{1,0:T(8,128)(2,1)S(1)} %get-tuple-element.39), channel_id=1, source_target_pairs={{0,1},{1,0},{2,3},{3,2},{4,5},{5,4},{6,7},{7,6},{8,9},{9,8},{10,11... | collective-permute-start | bytes 196616 | tf_op jit(solution)/shard_map/ppermute | solution.py:40
  8.9 7.2 %collective-permute-start.12 = (bf16[8,4096]{1,0:T(8,128)(2,1)S(1)}, bf16[8,4096]{1,0:T(8,128)(2,1)S(1)}, u32[]{:S(2)}, u32[]{:S(2)}) collective-permute-start(bf16[8,4096]{1,0:T(8,128)(2,1)S(1)} %get-tuple-element.41), channel_id=1, source_target_pairs={{0,25},{1,24},{2,27},{3,26},{4,29},{5,28},{6,31},{7,30},{8,17},{9,... | collective-permute-start | bytes 196616 | tf_op jit(solution)/shard_map/ppermute | solution.py:40
  8.9 8.1 %collective-permute-start.10 = (bf16[8,4096]{1,0:T(8,128)(2,1)S(1)}, bf16[8,4096]{1,0:T(8,128)(2,1)S(1)}, u32[]{:S(2)}, u32[]{:S(2)}) collective-permute-start(bf16[8,4096]{1,0:T(8,128)(2,1)S(1)} %get-tuple-element.36), channel_id=1, source_target_pairs={{0,17},{1,16},{2,19},{3,18},{4,21},{5,20},{6,23},{7,22},{8,25},{9,... | collective-permute-start | bytes 196616 | tf_op jit(solution)/shard_map/ppermute | solution.py:40
  11.2 7.0 %collective-permute-start.4 = (bf16[8,4096]{1,0:T(8,128)(2,1)S(1)}, bf16[8,4096]{1,0:T(8,128)(2,1)S(1)}, u32[]{:S(2)}, u32[]{:S(2)}) collective-permute-start(bf16[8,4096]{1,0:T(8,128)(2,1)S(1)} %get-tuple-element.36), channel_id=1, source_target_pairs={{0,16},{1,17},{2,18},{3,19},{4,20},{5,21},{6,22},{7,23},{8,24},{9,... | collective-permute-start | bytes 196616 | tf_op jit(solution)/shard_map/ppermute | solution.py:40
  13.8 4.9 %collective-permute-start.8 = (bf16[8,4096]{1,0:T(8,128)(2,1)S(1)}, bf16[8,4096]{1,0:T(8,128)(2,1)S(1)}, u32[]{:S(2)}, u32[]{:S(2)}) collective-permute-start(bf16[8,4096]{1,0:T(8,128)(2,1)S(1)} %get-tuple-element.40), channel_id=1, source_target_pairs={{0,1},{1,0},{2,3},{3,2},{4,5},{5,4},{6,7},{7,6},{8,9},{9,8},{10,11... | collective-permute-start | bytes 196616 | tf_op jit(solution)/shard_map/ppermute | solution.py:40
  15.4 5.2 %collective-permute-start.13 = (bf16[8,4096]{1,0:T(8,128)(2,1)S(1)}, bf16[8,4096]{1,0:T(8,128)(2,1)S(1)}, u32[]{:S(2)}, u32[]{:S(2)}) collective-permute-start(bf16[8,4096]{1,0:T(8,128)(2,1)S(1)} %get-tuple-element.42), channel_id=1, source_target_pairs={{0,25},{1,24},{2,27},{3,26},{4,29},{5,28},{6,31},{7,30},{8,17},{9,... | collective-permute-start | bytes 196616 | tf_op jit(solution)/shard_map/ppermute | solution.py:40
  16.1 9.3 %collective-permute-start.6 = (bf16[16,4096]{1,0:T(8,128)(2,1)S(1)}, bf16[16,4096]{1,0:T(8,128)(2,1)S(1)}, u32[]{:S(2)}, u32[]{:S(2)}) collective-permute-start(bf16[16,4096]{1,0:T(8,128)(2,1)S(1)} %get-tuple-element.38), channel_id=1, source_target_pairs={{0,24},{1,25},{2,26},{3,27},{4,28},{5,29},{6,30},{7,31},{8,16},{9,... | collective-permute-start | bytes 393224 | tf_op jit(solution)/shard_map/ppermute | solution.py:40
  17.1 8.3 %collective-permute-start.9 = (bf16[16,4096]{1,0:T(8,128)(2,1)S(1)}, bf16[16,4096]{1,0:T(8,128)(2,1)S(1)}, u32[]{:S(2)}, u32[]{:S(2)}) collective-permute-start(bf16[16,4096]{1,0:T(8,128)(2,1)S(1)} %get-tuple-element.35), channel_id=1, source_target_pairs={{0,9},{1,8},{2,11},{3,10},{4,13},{5,12},{6,15},{7,14},{8,1},{9,0},... | collective-permute-start | bytes 393224 | tf_op jit(solution)/shard_map/ppermute | solution.py:40
  18.1 7.2 %collective-permute-start.3 = (bf16[16,4096]{1,0:T(8,128)(2,1)S(1)}, bf16[16,4096]{1,0:T(8,128)(2,1)S(1)}, u32[]{:S(2)}, u32[]{:S(2)}) collective-permute-start(bf16[16,4096]{1,0:T(8,128)(2,1)S(1)} %get-tuple-element.35), channel_id=1, source_target_pairs={{0,8},{1,9},{2,10},{3,11},{4,12},{5,13},{6,14},{7,15},{8,0},{9,1},... | collective-permute-start | bytes 393224 | tf_op jit(solution)/shard_map/ppermute | solution.py:40
  18.7 6.5 %collective-permute-start.11 = (bf16[8,4096]{1,0:T(8,128)(2,1)S(1)}, bf16[8,4096]{1,0:T(8,128)(2,1)S(1)}, u32[]{:S(2)}, u32[]{:S(2)}) collective-permute-start(bf16[8,4096]{1,0:T(8,128)(2,1)S(1)} %get-tuple-element.37), channel_id=1, source_target_pairs={{0,17},{1,16},{2,19},{3,18},{4,21},{5,20},{6,23},{7,22},{8,25},{9,... | collective-permute-start | bytes 196616 | tf_op jit(solution)/shard_map/ppermute | solution.py:40
  20.6 4.8 %collective-permute-start.5 = (bf16[8,4096]{1,0:T(8,128)(2,1)S(1)}, bf16[8,4096]{1,0:T(8,128)(2,1)S(1)}, u32[]{:S(2)}, u32[]{:S(2)}) collective-permute-start(bf16[8,4096]{1,0:T(8,128)(2,1)S(1)} %get-tuple-element.37), channel_id=1, source_target_pairs={{0,16},{1,17},{2,18},{3,19},{4,20},{5,21},{6,22},{7,23},{8,24},{9,... | collective-permute-start | bytes 196616 | tf_op jit(solution)/shard_map/ppermute | solution.py:40
  25.4 14.7 %copy-start.3 = (bf16[4096,4]{0,1:T(4,128)(2,1)S(1)}, bf16[4096,4]{0,1:T(4,128)(2,1)}, u32[]{:S(2)}) copy-start(bf16[4096,4]{0,1:T(4,128)(2,1)} %param.7) | copy-start | bytes 98308
  33.5 4.3 %collective-permute-start.22 = (bf16[8,4096]{1,0:T(8,128)(2,1)S(1)}, bf16[8,4096]{1,0:T(8,128)(2,1)S(1)}, u32[]{:S(2)}, u32[]{:S(2)}) collective-permute-start(bf16[8,4096]{1,0:T(8,128)(2,1)S(1)} %get-tuple-element.55), channel_id=1, source_target_pairs={{0,16},{1,17},{2,18},{3,19},{4,20},{5,21},{6,22},{7,23},{8,24},{9,... | collective-permute-start | bytes 196616 | tf_op jit(solution)/shard_map/ppermute | solution.py:40
  34.9 5.1 %collective-permute-start.23 = (bf16[8,4096]{1,0:T(8,128)(2,1)S(1)}, bf16[8,4096]{1,0:T(8,128)(2,1)S(1)}, u32[]{:S(2)}, u32[]{:S(2)}) collective-permute-start(bf16[8,4096]{1,0:T(8,128)(2,1)S(1)} %get-tuple-element.56), channel_id=1, source_target_pairs={{0,1},{1,0},{2,3},{3,2},{4,5},{5,4},{6,7},{7,6},{8,9},{9,8},{10,11... | collective-permute-start | bytes 196616 | tf_op jit(solution)/shard_map/ppermute | solution.py:40
  36.2 9.9 %collective-permute-start.14 = (bf16[16,4096]{1,0:T(8,128)(2,1)S(1)}, bf16[16,4096]{1,0:T(8,128)(2,1)S(1)}, u32[]{:S(2)}, u32[]{:S(2)}) collective-permute-start(bf16[16,4096]{1,0:T(8,128)(2,1)S(1)} %get-tuple-element.44), channel_id=1, source_target_pairs={{0,8},{1,9},{2,10},{3,11},{4,12},{5,13},{6,14},{7,15},{8,0},{9,1},... | collective-permute-start | bytes 393224 | tf_op jit(solution)/shard_map/ppermute | solution.py:40
  36.2 11.1 %collective-permute-start.16 = (bf16[16,4096]{1,0:T(8,128)(2,1)S(1)}, bf16[16,4096]{1,0:T(8,128)(2,1)S(1)}, u32[]{:S(2)}, u32[]{:S(2)}) collective-permute-start(bf16[16,4096]{1,0:T(8,128)(2,1)S(1)} %get-tuple-element.46), channel_id=1, source_target_pairs={{0,24},{1,25},{2,26},{3,27},{4,28},{5,29},{6,30},{7,31},{8,16},{9,... | collective-permute-start | bytes 393224 | tf_op jit(solution)/shard_map/ppermute | solution.py:40
  37.0 11.4 %collective-permute-start.18 = (bf16[16,4096]{1,0:T(8,128)(2,1)S(1)}, bf16[16,4096]{1,0:T(8,128)(2,1)S(1)}, u32[]{:S(2)}, u32[]{:S(2)}) collective-permute-start(bf16[16,4096]{1,0:T(8,128)(2,1)S(1)} %get-tuple-element.48), channel_id=1, source_target_pairs={{0,9},{1,8},{2,11},{3,10},{4,13},{5,12},{6,15},{7,14},{8,1},{9,0},... | collective-permute-start | bytes 393224 | tf_op jit(solution)/shard_map/ppermute | solution.py:40
  37.8 5.8 %collective-permute-start.24 = (bf16[8,4096]{1,0:T(8,128)(2,1)S(1)}, bf16[8,4096]{1,0:T(8,128)(2,1)S(1)}, u32[]{:S(2)}, u32[]{:S(2)}) collective-permute-start(bf16[8,4096]{1,0:T(8,128)(2,1)S(1)} %get-tuple-element.57), channel_id=1, source_target_pairs={{0,17},{1,16},{2,19},{3,18},{4,21},{5,20},{6,23},{7,22},{8,25},{9,... | collective-permute-start | bytes 196616 | tf_op jit(solution)/shard_map/ppermute | solution.py:40
  40.0 5.2 %collective-permute-start.25 = (bf16[8,4096]{1,0:T(8,128)(2,1)S(1)}, bf16[8,4096]{1,0:T(8,128)(2,1)S(1)}, u32[]{:S(2)}, u32[]{:S(2)}) collective-permute-start(bf16[8,4096]{1,0:T(8,128)(2,1)S(1)} %get-tuple-element.58), channel_id=1, source_target_pairs={{0,25},{1,24},{2,27},{3,26},{4,29},{5,28},{6,31},{7,30},{8,17},{9,... | collective-permute-start | bytes 196616 | tf_op jit(solution)/shard_map/ppermute | solution.py:40
  43.7 7.8 %collective-permute-start.15 = (bf16[8,4096]{1,0:T(8,128)(2,1)S(1)}, bf16[8,4096]{1,0:T(8,128)(2,1)S(1)}, u32[]{:S(2)}, u32[]{:S(2)}) collective-permute-start(bf16[8,4096]{1,0:T(8,128)(2,1)S(1)} %get-tuple-element.45), channel_id=1, source_target_pairs={{0,16},{1,17},{2,18},{3,19},{4,20},{5,21},{6,22},{7,23},{8,24},{9,... | collective-permute-start | bytes 196616 | tf_op jit(solution)/shard_map/ppermute | solution.py:40
  45.2 7.1 %collective-permute-start.17 = (bf16[8,4096]{1,0:T(8,128)(2,1)S(1)}, bf16[8,4096]{1,0:T(8,128)(2,1)S(1)}, u32[]{:S(2)}, u32[]{:S(2)}) collective-permute-start(bf16[8,4096]{1,0:T(8,128)(2,1)S(1)} %get-tuple-element.47), channel_id=1, source_target_pairs={{0,1},{1,0},{2,3},{3,2},{4,5},{5,4},{6,7},{7,6},{8,9},{9,8},{10,11... | collective-permute-start | bytes 196616 | tf_op jit(solution)/shard_map/ppermute | solution.py:40
  46.2 6.1 %collective-permute-start.19 = (bf16[8,4096]{1,0:T(8,128)(2,1)S(1)}, bf16[8,4096]{1,0:T(8,128)(2,1)S(1)}, u32[]{:S(2)}, u32[]{:S(2)}) collective-permute-start(bf16[8,4096]{1,0:T(8,128)(2,1)S(1)} %get-tuple-element.49), channel_id=1, source_target_pairs={{0,17},{1,16},{2,19},{3,18},{4,21},{5,20},{6,23},{7,22},{8,25},{9,... | collective-permute-start | bytes 196616 | tf_op jit(solution)/shard_map/ppermute | solution.py:40
  47.3 5.3 %collective-permute-start.20 = (bf16[8,4096]{1,0:T(8,128)(2,1)S(1)}, bf16[8,4096]{1,0:T(8,128)(2,1)S(1)}, u32[]{:S(2)}, u32[]{:S(2)}) collective-permute-start(bf16[8,4096]{1,0:T(8,128)(2,1)S(1)} %get-tuple-element.50), channel_id=1, source_target_pairs={{0,25},{1,24},{2,27},{3,26},{4,29},{5,28},{6,31},{7,30},{8,17},{9,... | collective-permute-start | bytes 196616 | tf_op jit(solution)/shard_map/ppermute | solution.py:40
  48.7 7.2 %collective-permute-start.26 = (bf16[8,4096]{1,0:T(8,128)(2,1)S(1)}, bf16[8,4096]{1,0:T(8,128)(2,1)S(1)}, u32[]{:S(2)}, u32[]{:S(2)}) collective-permute-start(bf16[8,4096]{1,0:T(8,128)(2,1)S(1)} %get-tuple-element.61), channel_id=1, source_target_pairs={{0,4},{1,5},{2,6},{3,7},{4,0},{5,1},{6,2},{7,3},{8,12},{9,13},{10,... | collective-permute-start | bytes 196616 | tf_op jit(solution)/shard_map/ppermute | solution.py:40
  51.5 6.7 %collective-permute-start.27 = (bf16[8,4096]{1,0:T(8,128)(2,1)S(1)}, bf16[8,4096]{1,0:T(8,128)(2,1)S(1)}, u32[]{:S(2)}, u32[]{:S(2)}) collective-permute-start(bf16[8,4096]{1,0:T(8,128)(2,1)S(1)} %get-tuple-element.62), channel_id=1, source_target_pairs={{0,6},{1,7},{2,4},{3,5},{4,2},{5,3},{6,0},{7,1},{8,14},{9,15},{10,... | collective-permute-start | bytes 196616 | tf_op jit(solution)/shard_map/ppermute | solution.py:40
  52.9 6.0 %collective-permute-start.21 = (bf16[8,4096]{1,0:T(8,128)(2,1)S(1)}, bf16[8,4096]{1,0:T(8,128)(2,1)S(1)}, u32[]{:S(2)}, u32[]{:S(2)}) collective-permute-start(bf16[8,4096]{1,0:T(8,128)(2,1)S(1)} %get-tuple-element.54), channel_id=1, source_target_pairs={{0,2},{1,3},{2,0},{3,1},{4,6},{5,7},{6,4},{7,5},{8,10},{9,11},{10,... | collective-permute-start | bytes 196616 | tf_op jit(solution)/shard_map/ppermute | solution.py:40
